TPU v7x, 32 devices: a whole 2x2x4 slice. The times are simulated.
32 devices in a mesh: grp: 4 (over y, x), dev: 8 (over z, core).
Axes of the slice: x: 2, y: 2, z: 4, core: 2. Of those that a mesh axis runs over, the one named last changes fastest.
Arguments:
- obs_coord: float32 [3, 131072], P(None, ('grp', 'dev')), may hold values from -1 to 1
- obs_resid: float32 [131072], P(('grp', 'dev')), may hold values from -6 to 6
- obs_weight: float32 [131072], P(('grp', 'dev')), may hold values from 0.5 to 2
- obs_dest: int32 [131072], P(('grp', 'dev')), may hold values from 0 to 7, as said below
- obs_send_slot: int32 [131072], P(('grp', 'dev')), may hold values from 0 to 1023, as said below
- obs_elem: int32 [131072], P(('grp', 'dev')), may hold values from 0 to 255, as said below
- obs_slot: int32 [131072], P(('grp', 'dev')), may hold values from 0 to 31, as said below
Outputs:
- nodal: float32 [16, 64, 8, 512], P('grp', 'dev')
- total_cost: float32 [], replicated
Inputs may be any that keep to these rules, and one draw needn't show every extreme that they name: `obs_dest`: from the rows of one device, at most 1024 observations go to any one destination; in every group one destination receives exactly 1024 from every device of the group. `obs_send_slot`: distinct among the rows of one device with the same obs_dest. `obs_elem`: together with obs_slot distinct among all observations of a group with the same obs_dest. `obs_slot`: on every destination some element uses all 32 slots.
All inputs are finite; a program needn't handle non-finite values.
Results may differ from a plain program's by a relative error of at most 0.00017.
Values sent between devices are 32-bit elements; how exact they have to be, the bound alone decides.
A program may use at most 64 MiB of HBM per device.

v0:
```python
import functools
import math

import jax
import jax.numpy as jnp
from jax import lax
from jax.experimental import pallas as pl
from jax.experimental.pallas import tpu as pltpu
from jax.sharding import PartitionSpec as P

EX = 4
EY = 8
EZ = 8
ELEM_DEV = 256
LANES = 128
CHUNK = 1024
MESH = pl.DeviceIdType.MESH
F32 = jnp.float32
BF16 = jnp.bfloat16

ANCHORS = [-math.cos(math.pi * k / 7) for k in range(8)]
OUTER_PAIRS = [(a, b) for a in (0, 7) for b in range(8)]
OUTER_PAIRS += [(a, b) for a in range(1, 7) for b in (0, 7)]
INNER_PAIRS = [(a, b) for a in range(1, 7) for b in range(1, 7)]
PAIRS = OUTER_PAIRS + INNER_PAIRS
COEFS = [
    1.0 / math.prod(ANCHORS[a] - ANCHORS[m] for m in range(8) if m != a) for a in range(8)
]


def basis_values(t):
    factors = [t - p for p in ANCHORS]
    prefix = [None] * 8
    suffix = [None] * 8
    for k in range(1, 8):
        prefix[k] = factors[k - 1] if k == 1 else prefix[k - 1] * factors[k - 1]
    for k in range(6, -1, -1):
        suffix[k] = factors[k + 1] if k == 6 else suffix[k + 1] * factors[k + 1]
    basis = []
    for a in range(8):
        if a == 0:
            product = suffix[0]
        elif a == 7:
            product = prefix[7]
        else:
            product = prefix[a] * suffix[a]
        basis.append(product * COEFS[a])
    return basis


def dot_nt(left, right):
    return lax.dot_general(left, right, (((1,), (1,)), ((), ())), preferred_element_type=F32)


def split3(value):
    first = value.astype(BF16).astype(F32)
    rest = value - first
    second = rest.astype(BF16).astype(F32)
    return first, second, rest - second


def kernel(
    dev_count, grp_count, capacity,
    coord_in, resid_in, weight_in, dest_in, slot_in, elem_in,
    out, cost,
    coord, resid, weight, dest, slot, elem, acc, send, recv, cost_send, cost_recv, group_send, group_recv,
    third, outer, p_high, p_low, onehot, raw, a_send, a_recv, b_send, b_recv,
    send_sem, recv_sem, cost_send_sem, cost_recv_sem, group_send_sem, group_recv_sem,
    face_send_sem, face_recv_sem, edge_recv, edge_send_sem, edge_recv_sem, load_sem,
    face_rows, inner_rows,
):
    g = lax.axis_index("grp")
    d = lax.axis_index("dev")
    row_count = resid.shape[1]
    row_total = 2 * row_count // LANES
    per_dest = capacity // LANES
    per_chunk = 8 // per_dest

    def peer_of(k):
        peer, bit = 0, 1
        while bit < dev_count:
            peer = peer + lax.rem(d // bit + k // bit, 2) * bit
            bit *= 2
        return peer

    def wrapped(step_g, step_d):
        return (
            lax.rem(g + step_g + grp_count, grp_count),
            lax.rem(d + step_d + dev_count, dev_count),
        )

    barrier = pltpu.get_barrier_semaphore()
    partners = [(g, peer_of(k)) for k in range(1, dev_count)]
    partners += [wrapped(j, 0) for j in range(1, grp_count)]
    partners += [wrapped(i, j) for i in (-1, 1) for j in (-1, 1)]
    for partner in partners:
        pl.semaphore_signal(barrier, inc=1, device_id=partner, device_id_type=MESH)

    loads = [
        pltpu.make_async_copy(source, sink, load_sem.at[i])
        for i, (source, sink) in enumerate(
            zip(
                (dest_in, slot_in, resid_in, weight_in, coord_in, elem_in),
                (dest, slot, resid, weight, coord, elem),
            )
        )
    ]
    for load in loads:
        load.start()
    for load in loads:
        load.wait()

    acc[...] = jnp.zeros_like(acc)

    def pack(k, total):
        columns = pl.ds(pl.multiple_of(k * CHUNK, CHUNK), CHUNK)
        target = dest[:, columns] * capacity + slot[:, columns]
        high = jnp.broadcast_to(target // LANES, (row_total, CHUNK))
        low = jnp.broadcast_to(target % LANES, (LANES, CHUNK))
        row_hot = jnp.where(
            lax.broadcasted_iota(jnp.int32, (row_total, CHUNK), 0) == high, 1.0, 0.0
        ).astype(BF16)
        lane_hot = jnp.where(
            lax.broadcasted_iota(jnp.int32, (LANES, CHUNK), 0) == low, 1.0, 0.0
        ).astype(BF16)
        residual = resid[:, columns]
        forcing = weight[:, columns] * residual
        values = [coord[c : c + 1, columns] for c in range(3)] + [forcing]
        terms = [split3(value) for value in values]

        def spread(row):
            tile = jnp.broadcast_to(row, (16, CHUNK)).astype(BF16)
            return [row_hot[16 * i : 16 * i + 16] * tile for i in range(row_total // 16)]

        for t in range(3):
            pieces = []
            for channel in range(4):
                pieces += spread(terms[channel][t])
            if t == 0:
                pieces += spread(elem[:, columns].astype(F32))
            left = jnp.concatenate(pieces, axis=0)
            acc[0 : left.shape[0], :] += dot_nt(left, lane_hot)
        return total + forcing * residual

    total = lax.fori_loop(0, row_count // CHUNK, pack, jnp.zeros((1, CHUNK), F32), unroll=True)
    part = jnp.broadcast_to(0.5 * jnp.sum(total, axis=1, keepdims=True), (1, LANES))
    cost_send[...] = part
    for p in range(dev_count):
        for c in range(5):
            start = c * row_total + p * per_dest
            send[p, c * per_dest : (c + 1) * per_dest, :] = acc[start : start + per_dest, :]

    pl.semaphore_wait(barrier, len(partners))

    def data_copy(j):
        peer = peer_of(j)
        return pltpu.make_async_remote_copy(
            src_ref=send.at[peer], dst_ref=recv.at[j],
            send_sem=send_sem.at[j], recv_sem=recv_sem.at[j],
            device_id=(g, peer), device_id_type=MESH,
        )

    def cost_copy(j):
        return pltpu.make_async_remote_copy(
            src_ref=cost_send, dst_ref=cost_recv.at[j],
            send_sem=cost_send_sem.at[j], recv_sem=cost_recv_sem.at[j],
            device_id=(g, peer_of(j)), device_id_type=MESH,
        )

    def group_copy(j):
        return pltpu.make_async_remote_copy(
            src_ref=group_send, dst_ref=group_recv.at[j],
            send_sem=group_send_sem.at[j], recv_sem=group_recv_sem.at[j],
            device_id=wrapped(j, 0), device_id_type=MESH,
        )

    for j in range(1, dev_count):
        cost_copy(j).start()
    for j in range(1, dev_count):
        data_copy(j).start()
    recv[0] = send[d]

    face_rows[...] = jnp.zeros_like(face_rows)
    inner_rows[...] = jnp.zeros_like(inner_rows)

    def products(k, h, pairs):
        count = pairs.stop - pairs.start
        lanes = slice(h * LANES, (h + 1) * LANES)
        product = outer[k, pairs, h : h + 1, :] * third[k, :, h, :][None]
        product = product.reshape(count * 8, LANES)
        rounded = product.astype(BF16)
        p_high[0 : count * 8, lanes] = rounded
        p_low[0 : count * 8, lanes] = (product - rounded.astype(F32)).astype(BF16)

    def add_sums(k, sums):
        rows = slice(0, sums.shape[0])
        sums[...] += dot_nt(p_high[rows], onehot[k]) + dot_nt(p_low[rows], onehot[k])

    def element_sums(k, carry):
        for i in range(per_chunk):
            @pl.when(k * per_chunk + i > 0)
            def _():
                data_copy(k * per_chunk + i).wait_recv()

        def channel(c):
            rows = [
                recv[k * per_chunk + i, c * per_dest : (c + 1) * per_dest, :]
                for i in range(per_chunk)
            ]
            return rows[0] if per_chunk == 1 else jnp.concatenate(rows, axis=0)

        first_w = basis_values(channel(0))
        second_w = basis_values(channel(1))
        third_w = basis_values(channel(2))
        forcing = channel(3)
        owner = channel(4).astype(jnp.int32)
        weighted = [first * forcing for first in first_w]
        for c in range(8):
            third[k, c] = third_w[c]
        for i, (a, b) in enumerate(PAIRS):
            outer[k, i] = weighted[a] * second_w[b]
        ids = lax.broadcasted_iota(jnp.int32, (ELEM_DEV, LANES), 0)
        for h in range(8):
            products(k, h, slice(0, len(OUTER_PAIRS)))
            onehot[k, :, h * LANES : (h + 1) * LANES] = jnp.where(
                ids == jnp.broadcast_to(owner[h : h + 1, :], (ELEM_DEV, LANES)), 1.0, 0.0
            ).astype(BF16)
        add_sums(k, face_rows)
        return carry

    chunk_count = dev_count // per_chunk
    lax.fori_loop(0, chunk_count, element_sums, 0)

    def place(sums, pairs):
        for i, (a, b) in enumerate(pairs):
            start = a * 64 + b * 8
            raw[start : start + 8, :] = sums[i * 8 : i * 8 + 8, :]

    place(face_rows, OUTER_PAIRS)

    lane = lax.broadcasted_iota(jnp.int32, (1, LANES), 1)
    lower_half = lane < 64
    node = (lane // 8) % 8
    block = raw[448:512, 128:256]
    a_send[0] = jnp.where(lower_half, pltpu.roll(block[0:32], 64, 1), block[32:64])
    block = raw[0:64, 0:128]
    a_send[1] = jnp.where(lower_half, block[0:32], pltpu.roll(block[32:64], 64, 1))
    for half in range(2):
        columns = slice(half * LANES, (half + 1) * LANES)
        up = pltpu.roll(raw[56:64, columns], 72, 1)
        down = raw[0:8, columns]
        for a in range(1, 8):
            high = raw[a * 64 + 56 : a * 64 + 64, columns]
            low = raw[a * 64 : a * 64 + 8, columns]
            up = jnp.where(node == a, pltpu.roll(high, (a * 8 + 72) % 128, 1), up)
            down = jnp.where(node == a, pltpu.roll(low, a * 8, 1), down)
        b_send[0, half] = up
        b_send[1, half] = down

    steps = (1, -1)

    def face_copy(i):
        if i < 2:
            source, sink, target = a_send.at[i], a_recv.at[i], wrapped(steps[i], 0)
        else:
            source, sink, target = b_send.at[i - 2], b_recv.at[i - 2], wrapped(0, steps[i - 2])
        return pltpu.make_async_remote_copy(
            src_ref=source, dst_ref=sink,
            send_sem=face_send_sem.at[i], recv_sem=face_recv_sem.at[i],
            device_id=target, device_id_type=MESH,
        )

    def edge_copy(i, j):
        return pltpu.make_async_remote_copy(
            src_ref=b_send.at[j, 1 - i], dst_ref=edge_recv.at[j, i],
            send_sem=edge_send_sem.at[j, i], recv_sem=edge_recv_sem.at[j, i],
            device_id=wrapped(steps[i], steps[j]), device_id_type=MESH,
        )

    sends_a, sends_b = (g < grp_count - 1, g > 0), (d < dev_count - 1, d > 0)
    gets_a, gets_b = (g > 0, g < grp_count - 1), (d > 0, d < dev_count - 1)

    def when(condition, action):
        @pl.when(condition)
        def _():
            action()

    def clear(ref, i):
        ref[i] = jnp.zeros_like(ref[i])

    for j in range(2):
        for i in range(2):
            when(sends_a[i] & sends_b[j], lambda: edge_copy(i, j).start())
    for i in range(2):
        when(sends_a[i], lambda: face_copy(i).start())
        when(sends_b[i], lambda: face_copy(2 + i).start())

    group_cost = cost_send[...]
    for j in range(1, dev_count):
        cost_copy(j).wait_recv()
        group_cost = group_cost + cost_recv[j]
    group_send[...] = group_cost
    for j in range(1, grp_count):
        group_copy(j).start()

    def inner_sums(k, carry):
        for h in range(8):
            products(k, h, slice(len(OUTER_PAIRS), len(PAIRS)))
        add_sums(k, inner_rows)
        return carry

    lax.fori_loop(0, chunk_count, inner_sums, 0)
    place(inner_rows, INNER_PAIRS)

    for i in range(2):
        when(gets_a[i], lambda: face_copy(i).wait_recv())
        when(jnp.logical_not(gets_a[i]), lambda: clear(a_recv, i))
    low, high = raw[0:64, :], raw[448:512, :]
    from_low, from_high = a_recv[0], a_recv[1]
    from_low = jnp.concatenate([from_low, pltpu.roll(from_low, 64, 1)], axis=0)
    from_high = jnp.concatenate([pltpu.roll(from_high, 64, 1), from_high], axis=0)
    high_rolled = [pltpu.roll(high[:, :128], 64, 1), pltpu.roll(high[:, 128:], 64, 1)]
    low_rolled = [pltpu.roll(low[:, :128], 64, 1), pltpu.roll(low[:, 128:], 64, 1)]
    raw[0:64, 0:128] = low[:, :128] + jnp.where(lower_half, from_low, high_rolled[0])
    raw[0:64, 128:256] = low[:, 128:] + jnp.where(lower_half, high_rolled[0], high_rolled[1])
    raw[448:512, 0:128] = high[:, :128] + jnp.where(lower_half, low_rolled[0], low_rolled[1])
    raw[448:512, 128:256] = high[:, 128:] + jnp.where(lower_half, low_rolled[1], from_high)

    faces = []
    for j in range(2):
        when(gets_b[j], lambda: face_copy(2 + j).wait_recv())
        when(jnp.logical_not(gets_b[j]), lambda: clear(b_recv, j))
        for i in range(2):
            both = gets_a[i] & gets_b[j]
            when(both, lambda: edge_copy(i, j).wait_recv())
            when(jnp.logical_not(both), lambda: clear(edge_recv, (j, i)))
        first, second = b_recv[j, 0], b_recv[j, 1]
        up = [pltpu.roll(x, 8, 1) for x in (edge_recv[j, 0], first, second)]
        down = [pltpu.roll(x, 120, 1) for x in (first, second, edge_recv[j, 1])]
        face = []
        for half, own in enumerate((first, second)):
            from_low = jnp.where(lower_half, up[half], up[half + 1])
            from_high = jnp.where(lower_half, down[half], down[half + 1])
            face.append(
                own + jnp.where(node == 0, from_low, jnp.where(node == 7, from_high, 0.0))
            )
        faces.append(face)
    for half in range(2):
        columns = slice(half * LANES, (half + 1) * LANES)
        for a in range(8):
            low_rows = slice(a * 64, a * 64 + 8)
            high_rows = slice(a * 64 + 56, a * 64 + 64)
            low, high = raw[low_rows, columns], raw[high_rows, columns]
            got_low = pltpu.roll(faces[0][half], (128 - a * 8) % 128, 1)
            got_high = pltpu.roll(faces[1][half], (56 - a * 8) % 128, 1)
            raw[low_rows, columns] = low + jnp.where(node == 0, got_low, pltpu.roll(high, 8, 1))
            raw[high_rows, columns] = high + jnp.where(node == 7, got_high, pltpu.roll(low, 120, 1))

    ez = lax.broadcasted_iota(jnp.int32, (1, 8, LANES), 2) % 8
    c = lax.broadcasted_iota(jnp.int32, (1, 8, LANES), 1)
    takes_low = (c == 0) & (ez > 0)
    takes_high = (c == 7) & (ez < 7)
    for half in range(2):
        for part in range(4):
            rows = slice(part * 128, (part + 1) * 128)
            field = raw[rows, half * LANES : (half + 1) * LANES].reshape(16, 8, LANES)
            below = pltpu.roll(pltpu.roll(field, 1, 2), 1, 1)
            above = pltpu.roll(pltpu.roll(field, 127, 2), 7, 1)
            field = field + jnp.where(takes_low, below, jnp.where(takes_high, above, 0.0))
            out[half * LANES : (half + 1) * LANES, rows] = field.reshape(128, LANES).T

    all_cost = group_send[...]
    for j in range(1, grp_count):
        group_copy(j).wait_recv()
        all_cost = all_cost + group_recv[j]
    cost[...] = all_cost

    for j in range(1, dev_count):
        data_copy(j).wait_send()
        cost_copy(j).wait_send()
    for j in range(1, grp_count):
        group_copy(j).wait_send()
    for i in range(2):
        when(sends_a[i], lambda: face_copy(i).wait_send())
        when(sends_b[i], lambda: face_copy(2 + i).wait_send())
        for j in range(2):
            when(sends_a[i] & sends_b[j], lambda: edge_copy(i, j).wait_send())


def on_device(obs_coord, obs_resid, obs_weight, obs_dest, obs_send_slot, obs_elem, obs_slot):
    dev_count = lax.axis_size("dev")
    grp_count = lax.axis_size("grp")
    row_count = obs_resid.shape[0]
    capacity = 2 * row_count // dev_count
    per_dest = capacity // LANES
    chunks = 2 * row_count // CHUNK
    vmem = pl.BlockSpec(memory_space=pltpu.VMEM)
    dma = pltpu.SemaphoreType.DMA
    rows = [x.reshape(1, row_count) for x in (obs_resid, obs_weight, obs_dest, obs_send_slot, obs_elem)]
    field, cost = pl.pallas_call(
        functools.partial(kernel, dev_count, grp_count, capacity),
        out_shape=(
            pltpu.VMEM((ELEM_DEV, 512), F32),
            pltpu.VMEM((1, LANES), F32),
        ),
        in_specs=[pl.BlockSpec(memory_space=pl.ANY)] * 6,
        out_specs=(vmem, vmem),
        scratch_shapes=[
            pltpu.VMEM((3, row_count), F32),
            pltpu.VMEM((1, row_count), F32),
            pltpu.VMEM((1, row_count), F32),
            pltpu.VMEM((1, row_count), jnp.int32),
            pltpu.VMEM((1, row_count), jnp.int32),
            pltpu.VMEM((1, row_count), jnp.int32),
            pltpu.VMEM((5 * 2 * row_count // LANES, LANES), F32),
            pltpu.VMEM((dev_count, 5 * per_dest, LANES), F32),
            pltpu.VMEM((dev_count, 5 * per_dest, LANES), F32),
            pltpu.VMEM((1, LANES), F32),
            pltpu.VMEM((dev_count, 1, LANES), F32),
            pltpu.VMEM((1, LANES), F32),
            pltpu.VMEM((grp_count, 1, LANES), F32),
            pltpu.VMEM((chunks, 8, 8, LANES), F32),
            pltpu.VMEM((chunks, 64, 8, LANES), F32),
            pltpu.VMEM((len(INNER_PAIRS) * 8, CHUNK), BF16),
            pltpu.VMEM((len(INNER_PAIRS) * 8, CHUNK), BF16),
            pltpu.VMEM((chunks, ELEM_DEV, CHUNK), BF16),
            pltpu.VMEM((512, ELEM_DEV), F32),
            pltpu.VMEM((2, 32, LANES), F32),
            pltpu.VMEM((2, 32, LANES), F32),
            pltpu.VMEM((2, 2, 8, LANES), F32),
            pltpu.VMEM((2, 2, 8, LANES), F32),
            dma((dev_count,)),
            dma((dev_count,)),
            dma((dev_count,)),
            dma((dev_count,)),
            dma((grp_count,)),
            dma((grp_count,)),
            dma((4,)),
            dma((4,)),
            pltpu.VMEM((2, 2, 8, LANES), F32),
            dma((2, 2)),
            dma((2, 2)),
            dma((6,)),
            pltpu.VMEM((len(OUTER_PAIRS) * 8, ELEM_DEV), F32),
            pltpu.VMEM((len(INNER_PAIRS) * 8, ELEM_DEV), F32),
        ],
        compiler_params=pltpu.CompilerParams(collective_id=0, has_side_effects=True),
    )(obs_coord, *rows)
    return field.reshape(EX, EY, EZ, 512), cost[0, 0]


def solution(mesh):
    placed = (
        P(None, ("grp", "dev")),
        P(("grp", "dev")),
        P(("grp", "dev")),
        P(("grp", "dev")),
        P(("grp", "dev")),
        P(("grp", "dev")),
        P(("grp", "dev")),
    )
    return jax.shard_map(
        on_device,
        mesh=mesh,
        in_specs=placed,
        out_specs=(P("grp", "dev", None, None), P()),
        check_vma=False,
    )
```

profile of v0, /device:TPU:0, one launch (start us, length us, event | category | flops | bytes accessed | tf_op | source)
XLA Modules:
  0.0 21.3 jit_solution(4982916550540519658)
XLA Ops:
  0.6 18.7 %shard_map.77 = (f32[256,512]{1,0:T(8,128)S(1)}, f32[1,128]{1,0:T(1,128)S(1)}) custom-call(f32[3,4096]{1,0:T(4,128)} %coord_in.1, f32[1,4096]{1,0:T(1,128)} %bitcast.10, f32[1,4096]{1,0:T(1,128)} %bitcast.11, s32[1,4096]{1,0:T(1,128)} %bitcast.12, s32[1,4096]{1,0:T(1,128)} %bitcast.13, s32[1,4096]{1,0:T(1,128)} %bitcast.14), custom_call_target="tpu_custom_call" | custom-call | tf_op jit(solution)/shard_map/pallas_call | solution.py:400
  19.4 0.8 %copy.10 = f32[4,8,8,512]{3,2,1,0:T(8,128)} copy(f32[4,8,8,512]{3,2,1,0:T(8,128)S(1)} %bitcast.8) | data formatting | bytes 1048576
where the time goes:
time: 21.6 us; the launch traced here: 21.3 us
  Pallas kernels  18.7 us (87%)
  between operations  1.8 us (8%)
  local copies, waits for them, and re-layouts  0.8 us (4%)
    pallas_call x1, Pallas kernels, on_device(): pl.pallas_call(functools.partial(kernel, dev_count, grp_count, capacity),...  18.7 us
    unnamed x1, local copies, waits for them, and re-layouts  0.8 us

commit v1 on v0

--- a/solution.py
+++ b/solution.py
@@ -14,6 +14,7 @@
 ELEM_DEV = 256
 LANES = 128
 CHUNK = 1024
+BATCHES = 4
 MESH = pl.DeviceIdType.MESH
 F32 = jnp.float32
 BF16 = jnp.bfloat16
@@ -52,49 +53,53 @@
     return lax.dot_general(left, right, (((1,), (1,)), ((), ())), preferred_element_type=F32)
 
 
-def split3(value):
+def split2(value):
     first = value.astype(BF16).astype(F32)
-    rest = value - first
-    second = rest.astype(BF16).astype(F32)
-    return first, second, rest - second
+    return first, (value - first).astype(BF16).astype(F32)
+
+
+def one_hot(row, ids):
+    tile = jnp.broadcast_to(row, (16, row.shape[1])).astype(BF16)
+    hot = [jnp.where(part == tile, jnp.ones((), BF16), jnp.zeros((), BF16)) for part in ids]
+    return hot[0] if len(hot) == 1 else jnp.concatenate(hot, axis=0)
+
+
+def sublane_ids(count):
+    ids = lax.broadcasted_iota(jnp.int32, (16, LANES), 0)
+    return [(ids + 16 * i).astype(F32).astype(BF16) for i in range(count // 16)]
 
 
 def kernel(
     dev_count, grp_count, capacity,
     coord_in, resid_in, weight_in, dest_in, slot_in, elem_in,
     out, cost,
-    coord, resid, weight, dest, slot, elem, acc, send, recv, cost_send, cost_recv, group_send, group_recv,
-    third, outer, p_high, p_low, onehot, raw, a_send, a_recv, b_send, b_recv,
+    coord, resid, weight, dest, slot, elem, terms, left, lane_hot, send, recv,
+    cost_send, cost_recv, group_send, group_recv,
+    third, outer, product, onehot, raw, a_send, a_recv, b_send, b_recv, edge_recv,
+    face_rows, inner_rows,
     send_sem, recv_sem, cost_send_sem, cost_recv_sem, group_send_sem, group_recv_sem,
-    face_send_sem, face_recv_sem, edge_recv, edge_send_sem, edge_recv_sem, load_sem,
-    face_rows, inner_rows,
+    face_send_sem, face_recv_sem, edge_send_sem, edge_recv_sem, load_sem,
+    up_sem, others_sem,
 ):
     g = lax.axis_index("grp")
     d = lax.axis_index("dev")
-    row_count = resid.shape[1]
-    row_total = 2 * row_count // LANES
+    obs_rows = resid.shape[0]
     per_dest = capacity // LANES
-    per_chunk = 8 // per_dest
-
-    def peer_of(k):
-        peer, bit = 0, 1
-        while bit < dev_count:
-            peer = peer + lax.rem(d // bit + k // bit, 2) * bit
-            bit *= 2
-        return peer
+    half_dev = dev_count // 2
+    row_total = half_dev * per_dest
+    batch = dev_count // BATCHES
+    per_block = 8 // per_dest
+
+    def when(condition, action):
+        @pl.when(condition)
+        def _():
+            action()
 
     def wrapped(step_g, step_d):
         return (
             lax.rem(g + step_g + grp_count, grp_count),
             lax.rem(d + step_d + dev_count, dev_count),
         )
-
-    barrier = pltpu.get_barrier_semaphore()
-    partners = [(g, peer_of(k)) for k in range(1, dev_count)]
-    partners += [wrapped(j, 0) for j in range(1, grp_count)]
-    partners += [wrapped(i, j) for i in (-1, 1) for j in (-1, 1)]
-    for partner in partners:
-        pl.semaphore_signal(barrier, inc=1, device_id=partner, device_id_type=MESH)
 
     loads = [
         pltpu.make_async_copy(source, sink, load_sem.at[i])
@@ -107,64 +112,84 @@
     ]
     for load in loads:
         load.start()
+
+    barrier = pltpu.get_barrier_semaphore()
+    others = [wrapped(j, 0) for j in range(1, grp_count)]
+    others += [wrapped(i, j) for i in (-1, 1) for j in (-1, 1)]
+
+    def signal(semaphore, partner):
+        pl.semaphore_signal(semaphore, inc=1, device_id=partner, device_id_type=MESH)
+
+    def is_lower(partner):
+        return (partner[1] < d) | ((partner[1] == d) & (partner[0] < g))
+
+    for p in range(dev_count):
+        when(p > d, lambda: signal(barrier, (g, p)))
+    lower_count = d
+    higher_others = len(others)
+    for partner in others:
+        lower = is_lower(partner)
+        when(jnp.logical_not(lower), lambda: signal(barrier, partner))
+        lower_count = lower_count + lower.astype(jnp.int32)
+        higher_others = higher_others - lower.astype(jnp.int32)
+    when(lower_count > 0, lambda: pl.semaphore_wait(barrier, lower_count))
+    for p in range(dev_count):
+        when(p < d, lambda: signal(up_sem.at[d], (g, p)))
+    for partner in others:
+        when(is_lower(partner), lambda: signal(others_sem, partner))
+
     for load in loads:
         load.wait()
 
-    acc[...] = jnp.zeros_like(acc)
-
-    def pack(k, total):
-        columns = pl.ds(pl.multiple_of(k * CHUNK, CHUNK), CHUNK)
-        target = dest[:, columns] * capacity + slot[:, columns]
-        high = jnp.broadcast_to(target // LANES, (row_total, CHUNK))
-        low = jnp.broadcast_to(target % LANES, (LANES, CHUNK))
-        row_hot = jnp.where(
-            lax.broadcasted_iota(jnp.int32, (row_total, CHUNK), 0) == high, 1.0, 0.0
-        ).astype(BF16)
-        lane_hot = jnp.where(
-            lax.broadcasted_iota(jnp.int32, (LANES, CHUNK), 0) == low, 1.0, 0.0
-        ).astype(BF16)
-        residual = resid[:, columns]
-        forcing = weight[:, columns] * residual
-        values = [coord[c : c + 1, columns] for c in range(3)] + [forcing]
-        terms = [split3(value) for value in values]
-
-        def spread(row):
-            tile = jnp.broadcast_to(row, (16, CHUNK)).astype(BF16)
-            return [row_hot[16 * i : 16 * i + 16] * tile for i in range(row_total // 16)]
-
-        for t in range(3):
-            pieces = []
-            for channel in range(4):
-                pieces += spread(terms[channel][t])
-            if t == 0:
-                pieces += spread(elem[:, columns].astype(F32))
-            left = jnp.concatenate(pieces, axis=0)
-            acc[0 : left.shape[0], :] += dot_nt(left, lane_hot)
-        return total + forcing * residual
-
-    total = lax.fori_loop(0, row_count // CHUNK, pack, jnp.zeros((1, CHUNK), F32), unroll=True)
-    part = jnp.broadcast_to(0.5 * jnp.sum(total, axis=1, keepdims=True), (1, LANES))
-    cost_send[...] = part
+    residual = resid[...]
+    forcing = weight[...] * residual
+    high, low = split2(forcing)
+    where = dest[...]
+    which = slot[...]
+    terms[0] = ((where % half_dev) * per_dest + which // LANES).astype(F32)
+    terms[1] = ((where // half_dev) * LANES + which % LANES).astype(F32)
+    terms[2] = high
+    terms[3] = low
+    terms[4] = elem[...].astype(F32)
+    part = jnp.sum(forcing * residual, axis=0, keepdims=True)
+    cost_send[...] = jnp.broadcast_to(0.5 * jnp.sum(part, axis=1, keepdims=True), (1, LANES))
+
+    row_ids = sublane_ids(row_total)
+    lane_ids = sublane_ids(2 * LANES)
+    for r in range(obs_rows):
+        columns = slice(r * LANES, (r + 1) * LANES)
+        row_hot = one_hot(terms[0, r : r + 1, :], row_ids)
+        lane_hot[:, columns] = one_hot(terms[1, r : r + 1, :], lane_ids)
+        coord_high, coord_low = split2(coord[:, columns])
+        values = [coord_high[c : c + 1] for c in range(3)] + [terms[2, r : r + 1, :]]
+        values += [terms[4, r : r + 1, :]]
+        values += [coord_low[c : c + 1] for c in range(3)] + [terms[3, r : r + 1, :]]
+        for i, value in enumerate(values):
+            tile = jnp.broadcast_to(value, (row_total, LANES)).astype(BF16)
+            left[i * row_total : (i + 1) * row_total, columns] = row_hot * tile
+    packed = dot_nt(left[...], lane_hot[...])
     for p in range(dev_count):
+        lanes = slice(p // half_dev * LANES, (p // half_dev + 1) * LANES)
         for c in range(5):
-            start = c * row_total + p * per_dest
-            send[p, c * per_dest : (c + 1) * per_dest, :] = acc[start : start + per_dest, :]
-
-    pl.semaphore_wait(barrier, len(partners))
-
-    def data_copy(j):
-        peer = peer_of(j)
+            start = c * row_total + p % half_dev * per_dest
+            rows = packed[start : start + per_dest, lanes]
+            if c < 4:
+                start = (c + 5) * row_total + p % half_dev * per_dest
+                rows = rows + packed[start : start + per_dest, lanes]
+            send[p, c * per_dest : (c + 1) * per_dest, :] = rows
+
+    def data_copy(p, source):
         return pltpu.make_async_remote_copy(
-            src_ref=send.at[peer], dst_ref=recv.at[j],
-            send_sem=send_sem.at[j], recv_sem=recv_sem.at[j],
-            device_id=(g, peer), device_id_type=MESH,
-        )
-
-    def cost_copy(j):
+            src_ref=send.at[p], dst_ref=recv.at[source],
+            send_sem=send_sem.at[p], recv_sem=recv_sem.at[source],
+            device_id=(g, p), device_id_type=MESH,
+        )
+
+    def cost_copy(p, source):
         return pltpu.make_async_remote_copy(
-            src_ref=cost_send, dst_ref=cost_recv.at[j],
-            send_sem=cost_send_sem.at[j], recv_sem=cost_recv_sem.at[j],
-            device_id=(g, peer_of(j)), device_id_type=MESH,
+            src_ref=cost_send, dst_ref=cost_recv.at[source],
+            send_sem=cost_send_sem.at[p], recv_sem=cost_recv_sem.at[source],
+            device_id=(g, p), device_id_type=MESH,
         )
 
     def group_copy(j):
@@ -174,62 +199,107 @@
             device_id=wrapped(j, 0), device_id_type=MESH,
         )
 
-    for j in range(1, dev_count):
-        cost_copy(j).start()
-    for j in range(1, dev_count):
-        data_copy(j).start()
-    recv[0] = send[d]
-
-    face_rows[...] = jnp.zeros_like(face_rows)
-    inner_rows[...] = jnp.zeros_like(inner_rows)
-
-    def products(k, h, pairs):
-        count = pairs.stop - pairs.start
-        lanes = slice(h * LANES, (h + 1) * LANES)
-        product = outer[k, pairs, h : h + 1, :] * third[k, :, h, :][None]
-        product = product.reshape(count * 8, LANES)
-        rounded = product.astype(BF16)
-        p_high[0 : count * 8, lanes] = rounded
-        p_low[0 : count * 8, lanes] = (product - rounded.astype(F32)).astype(BF16)
-
-    def add_sums(k, sums):
-        rows = slice(0, sums.shape[0])
-        sums[...] += dot_nt(p_high[rows], onehot[k]) + dot_nt(p_low[rows], onehot[k])
-
-    def element_sums(k, carry):
-        for i in range(per_chunk):
-            @pl.when(k * per_chunk + i > 0)
-            def _():
-                data_copy(k * per_chunk + i).wait_recv()
-
+    own = d // batch
+
+    def send_to(p):
+        when(p > d, lambda: pl.semaphore_wait(up_sem.at[p], 1))
+        data_copy(p, d).start()
+        cost_copy(p, d).start()
+
+    late = dev_count - batch
+    for p in range(late):
+        when(p != d, lambda: send_to(p))
+    for p in range(late, dev_count):
+        when((own == BATCHES - 1) & (p != d), lambda: send_to(p))
+    recv[d] = send[d]
+
+    def channels(x, j):
         def channel(c):
             rows = [
-                recv[k * per_chunk + i, c * per_dest : (c + 1) * per_dest, :]
-                for i in range(per_chunk)
+                recv[x * batch + j * per_block + i, c * per_dest : (c + 1) * per_dest, :]
+                for i in range(per_block)
             ]
-            return rows[0] if per_chunk == 1 else jnp.concatenate(rows, axis=0)
-
-        first_w = basis_values(channel(0))
-        second_w = basis_values(channel(1))
-        third_w = basis_values(channel(2))
-        forcing = channel(3)
-        owner = channel(4).astype(jnp.int32)
-        weighted = [first * forcing for first in first_w]
-        for c in range(8):
-            third[k, c] = third_w[c]
-        for i, (a, b) in enumerate(PAIRS):
-            outer[k, i] = weighted[a] * second_w[b]
-        ids = lax.broadcasted_iota(jnp.int32, (ELEM_DEV, LANES), 0)
-        for h in range(8):
-            products(k, h, slice(0, len(OUTER_PAIRS)))
-            onehot[k, :, h * LANES : (h + 1) * LANES] = jnp.where(
-                ids == jnp.broadcast_to(owner[h : h + 1, :], (ELEM_DEV, LANES)), 1.0, 0.0
-            ).astype(BF16)
-        add_sums(k, face_rows)
+            return rows[0] if per_block == 1 else jnp.concatenate(rows, axis=0)
+
+        return [channel(c) for c in range(5)]
+
+    elem_ids = sublane_ids(ELEM_DEV)
+    blocks = batch * capacity // CHUNK
+
+    def prepare(x):
+        for j in range(blocks):
+            u, v, w, forcing, owner = channels(x, j)
+            rows = slice(j * 8, j * 8 + 8)
+            second_w = basis_values(v)
+            weighted = [first * forcing for first in basis_values(u)]
+            for c, value in enumerate(basis_values(w)):
+                third[c, rows] = value
+            for i, (a, b) in enumerate(PAIRS):
+                outer[i, rows] = weighted[a] * second_w[b]
+            for h in range(8):
+                columns = slice((j * 8 + h) * LANES, (j * 8 + h + 1) * LANES)
+                onehot[:, columns] = one_hot(owner[h : h + 1, :], elem_ids)
+
+    face_count, inner_count = len(OUTER_PAIRS), len(INNER_PAIRS)
+
+    def products(pairs, start):
+        count = pairs.stop - pairs.start
+        for h in range(blocks * 8):
+            columns = slice(h * LANES, (h + 1) * LANES)
+            value = outer[pairs, h : h + 1, :] * third[:, h, :][None]
+            value = value.reshape(count * 8, LANES)
+            rounded = value.astype(BF16)
+            product[start : start + count * 8, columns] = rounded
+            rest = (value - rounded.astype(F32)).astype(BF16)
+            product[start + count * 8 : start + count * 16, columns] = rest
+
+    def face_products():
+        products(slice(0, face_count), 0)
+
+    def inner_products():
+        products(slice(face_count, len(PAIRS)), face_count * 16)
+
+    def add_rows(sums, total, first):
+        count = sums.shape[0]
+        value = total[0:count] + total[count : 2 * count]
+        if first:
+            sums[...] = value
+        else:
+            sums[...] += value
+
+    def all_rows(x, first):
+        prepare(x)
+        face_products()
+        inner_products()
+        total = dot_nt(product[...], onehot[...])
+        add_rows(face_rows, total[0 : face_count * 16], first)
+        add_rows(inner_rows, total[face_count * 16 :], first)
+
+    def arrive(source):
+        data_copy(source, source).wait_recv()
+
+    for i in range(batch):
+        when(own * batch + i != d, lambda: arrive(own * batch + i))
+    all_rows(own, True)
+
+    for p in range(late, dev_count):
+        when(own != BATCHES - 1, lambda: send_to(p))
+
+    def from_batch(t):
+        x = t - 1 + (t > own).astype(jnp.int32)
+        for i in range(batch):
+            arrive(x * batch + i)
+        return x
+
+    def middle(t, carry):
+        all_rows(from_batch(t), False)
         return carry
 
-    chunk_count = dev_count // per_chunk
-    lax.fori_loop(0, chunk_count, element_sums, 0)
+    lax.fori_loop(1, BATCHES - 1, middle, 0)
+    prepare(from_batch(BATCHES - 1))
+    face_products()
+    total = dot_nt(product[0 : face_count * 16], onehot[...])
+    add_rows(face_rows, total, False)
 
     def place(sums, pairs):
         for i, (a, b) in enumerate(pairs):
@@ -280,14 +350,10 @@
     sends_a, sends_b = (g < grp_count - 1, g > 0), (d < dev_count - 1, d > 0)
     gets_a, gets_b = (g > 0, g < grp_count - 1), (d > 0, d < dev_count - 1)
 
-    def when(condition, action):
-        @pl.when(condition)
-        def _():
-            action()
-
     def clear(ref, i):
         ref[i] = jnp.zeros_like(ref[i])
 
+    when(higher_others > 0, lambda: pl.semaphore_wait(others_sem, higher_others))
     for j in range(2):
         for i in range(2):
             when(sends_a[i] & sends_b[j], lambda: edge_copy(i, j).start())
@@ -296,20 +362,16 @@
         when(sends_b[i], lambda: face_copy(2 + i).start())
 
     group_cost = cost_send[...]
-    for j in range(1, dev_count):
-        cost_copy(j).wait_recv()
-        group_cost = group_cost + cost_recv[j]
+    for i in range(dev_count):
+        when(i != d, lambda: cost_copy(i, i).wait_recv())
+        group_cost = group_cost + jnp.where(i == d, 0.0, cost_recv[i])
     group_send[...] = group_cost
     for j in range(1, grp_count):
         group_copy(j).start()
 
-    def inner_sums(k, carry):
-        for h in range(8):
-            products(k, h, slice(len(OUTER_PAIRS), len(PAIRS)))
-        add_sums(k, inner_rows)
-        return carry
-
-    lax.fori_loop(0, chunk_count, inner_sums, 0)
+    inner_products()
+    total = dot_nt(product[face_count * 16 :], onehot[...])
+    add_rows(inner_rows, total, False)
     place(inner_rows, INNER_PAIRS)
 
     for i in range(2):
@@ -375,9 +437,9 @@
         all_cost = all_cost + group_recv[j]
     cost[...] = all_cost
 
-    for j in range(1, dev_count):
-        data_copy(j).wait_send()
-        cost_copy(j).wait_send()
+    for p in range(dev_count):
+        when(p != d, lambda: data_copy(p, p).wait_send())
+        when(p != d, lambda: cost_copy(p, p).wait_send())
     for j in range(1, grp_count):
         group_copy(j).wait_send()
     for i in range(2):
@@ -391,12 +453,18 @@
     dev_count = lax.axis_size("dev")
     grp_count = lax.axis_size("grp")
     row_count = obs_resid.shape[0]
+    obs_rows = row_count // LANES
     capacity = 2 * row_count // dev_count
     per_dest = capacity // LANES
-    chunks = 2 * row_count // CHUNK
+    packed_rows = dev_count // 2 * per_dest
+    batch_obs = dev_count // BATCHES * capacity
     vmem = pl.BlockSpec(memory_space=pltpu.VMEM)
     dma = pltpu.SemaphoreType.DMA
-    rows = [x.reshape(1, row_count) for x in (obs_resid, obs_weight, obs_dest, obs_send_slot, obs_elem)]
+    regular = pltpu.SemaphoreType.REGULAR
+    rows = [
+        x.reshape(obs_rows, LANES)
+        for x in (obs_resid, obs_weight, obs_dest, obs_send_slot, obs_elem)
+    ]
     field, cost = pl.pallas_call(
         functools.partial(kernel, dev_count, grp_count, capacity),
         out_shape=(
@@ -407,28 +475,32 @@
         out_specs=(vmem, vmem),
         scratch_shapes=[
             pltpu.VMEM((3, row_count), F32),
-            pltpu.VMEM((1, row_count), F32),
-            pltpu.VMEM((1, row_count), F32),
-            pltpu.VMEM((1, row_count), jnp.int32),
-            pltpu.VMEM((1, row_count), jnp.int32),
-            pltpu.VMEM((1, row_count), jnp.int32),
-            pltpu.VMEM((5 * 2 * row_count // LANES, LANES), F32),
+            pltpu.VMEM((obs_rows, LANES), F32),
+            pltpu.VMEM((obs_rows, LANES), F32),
+            pltpu.VMEM((obs_rows, LANES), jnp.int32),
+            pltpu.VMEM((obs_rows, LANES), jnp.int32),
+            pltpu.VMEM((obs_rows, LANES), jnp.int32),
+            pltpu.VMEM((5, obs_rows, LANES), F32),
+            pltpu.VMEM((9 * packed_rows, row_count), BF16),
+            pltpu.VMEM((2 * LANES, row_count), BF16),
             pltpu.VMEM((dev_count, 5 * per_dest, LANES), F32),
             pltpu.VMEM((dev_count, 5 * per_dest, LANES), F32),
             pltpu.VMEM((1, LANES), F32),
             pltpu.VMEM((dev_count, 1, LANES), F32),
             pltpu.VMEM((1, LANES), F32),
             pltpu.VMEM((grp_count, 1, LANES), F32),
-            pltpu.VMEM((chunks, 8, 8, LANES), F32),
-            pltpu.VMEM((chunks, 64, 8, LANES), F32),
-            pltpu.VMEM((len(INNER_PAIRS) * 8, CHUNK), BF16),
-            pltpu.VMEM((len(INNER_PAIRS) * 8, CHUNK), BF16),
-            pltpu.VMEM((chunks, ELEM_DEV, CHUNK), BF16),
+            pltpu.VMEM((8, batch_obs // LANES, LANES), F32),
+            pltpu.VMEM((64, batch_obs // LANES, LANES), F32),
+            pltpu.VMEM((1024, batch_obs), BF16),
+            pltpu.VMEM((ELEM_DEV, batch_obs), BF16),
             pltpu.VMEM((512, ELEM_DEV), F32),
             pltpu.VMEM((2, 32, LANES), F32),
             pltpu.VMEM((2, 32, LANES), F32),
             pltpu.VMEM((2, 2, 8, LANES), F32),
             pltpu.VMEM((2, 2, 8, LANES), F32),
+            pltpu.VMEM((2, 2, 8, LANES), F32),
+            pltpu.VMEM((len(OUTER_PAIRS) * 8, ELEM_DEV), F32),
+            pltpu.VMEM((len(INNER_PAIRS) * 8, ELEM_DEV), F32),
             dma((dev_count,)),
             dma((dev_count,)),
             dma((dev_count,)),
@@ -437,12 +509,11 @@
             dma((grp_count,)),
             dma((4,)),
             dma((4,)),
-            pltpu.VMEM((2, 2, 8, LANES), F32),
             dma((2, 2)),
             dma((2, 2)),
             dma((6,)),
-            pltpu.VMEM((len(OUTER_PAIRS) * 8, ELEM_DEV), F32),
-            pltpu.VMEM((len(INNER_PAIRS) * 8, ELEM_DEV), F32),
+            regular((dev_count,)),
+            regular,
         ],
         compiler_params=pltpu.CompilerParams(collective_id=0, has_side_effects=True),
     )(obs_coord, *rows)

time: 21.6 us -> 21.9 us (1.014)
  the two profiles are of different devices: /device:TPU:0 before, /device:TPU:19 now
where the time goes in v1:
time: 21.9 us; the launch traced here: 21.6 us
  Pallas kernels  19 us (87%)
  between operations  1.8 us (8%)
  local copies, waits for them, and re-layouts  0.8 us (4%)
    pallas_call x1, Pallas kernels, on_device(): pl.pallas_call(functools.partial(kernel, dev_count, grp_count, capacity),...  19 us
    unnamed x1, local copies, waits for them, and re-layouts  0.8 us

profile of v1, /device:TPU:19, one launch (start us, length us, event | category | flops | bytes accessed | tf_op | source)
XLA Modules:
  0.0 21.6 jit_solution(13524758951332748187)
XLA Ops:
  0.6 19.0 %shard_map.77 = (f32[256,512]{1,0:T(8,128)S(1)}, f32[1,128]{1,0:T(1,128)S(1)}) custom-call(f32[3,4096]{1,0:T(4,128)} %coord_in.1, f32[32,128]{1,0:T(8,128)} %bitcast.10, f32[32,128]{1,0:T(8,128)} %bitcast.11, s32[32,128]{1,0:T(8,128)} %bitcast.12, s32[32,128]{1,0:T(8,128)} %bitcast.13, s32[32,128]{1,0:T(8,128)} %bitcast.14), custom_call_target="tpu_custom_call" | custom-call | tf_op jit(solution)/shard_map/pallas_call | solution.py:468
  19.7 0.8 %copy.10 = f32[4,8,8,512]{3,2,1,0:T(8,128)} copy(f32[4,8,8,512]{3,2,1,0:T(8,128)S(1)} %bitcast.8) | data formatting | bytes 1048576

commit v2 on v1

--- a/solution.py
+++ b/solution.py
@@ -13,7 +13,8 @@
 EZ = 8
 ELEM_DEV = 256
 LANES = 128
-CHUNK = 1024
+SLOTS = 32
+CHANNELS = 6
 BATCHES = 4
 MESH = pl.DeviceIdType.MESH
 F32 = jnp.float32
@@ -53,15 +54,19 @@
     return lax.dot_general(left, right, (((1,), (1,)), ((), ())), preferred_element_type=F32)
 
 
-def split2(value):
-    first = value.astype(BF16).astype(F32)
-    return first, (value - first).astype(BF16).astype(F32)
+def halves(row):
+    value = jnp.broadcast_to(row, (16, LANES))
+    first = value.astype(BF16)
+    return first, (value - first.astype(F32)).astype(BF16)
 
 
 def one_hot(row, ids):
-    tile = jnp.broadcast_to(row, (16, row.shape[1])).astype(BF16)
-    hot = [jnp.where(part == tile, jnp.ones((), BF16), jnp.zeros((), BF16)) for part in ids]
-    return hot[0] if len(hot) == 1 else jnp.concatenate(hot, axis=0)
+    tile = jnp.broadcast_to(row, (16, LANES)).astype(BF16)
+    return [jnp.where(part == tile, jnp.ones((), BF16), jnp.zeros((), BF16)) for part in ids]
+
+
+def spread(hot, tiles):
+    return jnp.concatenate([part * tile for tile in tiles for part in hot], axis=0)
 
 
 def sublane_ids(count):
@@ -71,12 +76,11 @@
 
 def kernel(
     dev_count, grp_count, capacity,
-    coord_in, resid_in, weight_in, dest_in, slot_in, elem_in,
+    coord_in, resid_in, weight_in, dest_in, send_slot_in, elem_in, slot_in,
     out, cost,
-    coord, resid, weight, dest, slot, elem, terms, left, lane_hot, send, recv,
+    coord, resid, weight, dest, send_slot, elem, slot, terms, send, recv,
     cost_send, cost_recv, group_send, group_recv,
-    third, outer, product, onehot, raw, a_send, a_recv, b_send, b_recv, edge_recv,
-    face_rows, inner_rows,
+    grid, first, second, third, raw, a_send, a_recv, b_send, b_recv, edge_recv,
     send_sem, recv_sem, cost_send_sem, cost_recv_sem, group_send_sem, group_recv_sem,
     face_send_sem, face_recv_sem, edge_send_sem, edge_recv_sem, load_sem,
     up_sem, others_sem,
@@ -88,7 +92,6 @@
     half_dev = dev_count // 2
     row_total = half_dev * per_dest
     batch = dev_count // BATCHES
-    per_block = 8 // per_dest
 
     def when(condition, action):
         @pl.when(condition)
@@ -105,8 +108,8 @@
         pltpu.make_async_copy(source, sink, load_sem.at[i])
         for i, (source, sink) in enumerate(
             zip(
-                (dest_in, slot_in, resid_in, weight_in, coord_in, elem_in),
-                (dest, slot, resid, weight, coord, elem),
+                (dest_in, send_slot_in, resid_in, weight_in, coord_in, elem_in, slot_in),
+                (dest, send_slot, resid, weight, coord, elem, slot),
             )
         )
     ]
@@ -143,38 +146,36 @@
 
     residual = resid[...]
     forcing = weight[...] * residual
-    high, low = split2(forcing)
     where = dest[...]
-    which = slot[...]
+    which = send_slot[...]
     terms[0] = ((where % half_dev) * per_dest + which // LANES).astype(F32)
     terms[1] = ((where // half_dev) * LANES + which % LANES).astype(F32)
-    terms[2] = high
-    terms[3] = low
-    terms[4] = elem[...].astype(F32)
+    terms[2] = forcing
+    terms[3] = elem[...].astype(F32)
+    terms[4] = slot[...].astype(F32)
     part = jnp.sum(forcing * residual, axis=0, keepdims=True)
     cost_send[...] = jnp.broadcast_to(0.5 * jnp.sum(part, axis=1, keepdims=True), (1, LANES))
 
     row_ids = sublane_ids(row_total)
     lane_ids = sublane_ids(2 * LANES)
+    left, right = [], []
     for r in range(obs_rows):
         columns = slice(r * LANES, (r + 1) * LANES)
-        row_hot = one_hot(terms[0, r : r + 1, :], row_ids)
-        lane_hot[:, columns] = one_hot(terms[1, r : r + 1, :], lane_ids)
-        coord_high, coord_low = split2(coord[:, columns])
-        values = [coord_high[c : c + 1] for c in range(3)] + [terms[2, r : r + 1, :]]
-        values += [terms[4, r : r + 1, :]]
-        values += [coord_low[c : c + 1] for c in range(3)] + [terms[3, r : r + 1, :]]
-        for i, value in enumerate(values):
-            tile = jnp.broadcast_to(value, (row_total, LANES)).astype(BF16)
-            left[i * row_total : (i + 1) * row_total, columns] = row_hot * tile
-    packed = dot_nt(left[...], lane_hot[...])
+        values = [halves(coord[c : c + 1, columns]) for c in range(3)]
+        values.append(halves(terms[2, r : r + 1, :]))
+        tiles = [high for high, _ in values]
+        tiles += [halves(terms[i, r : r + 1, :])[0] for i in (3, 4)]
+        tiles += [low for _, low in values]
+        left.append(spread(one_hot(terms[0, r : r + 1, :], row_ids), tiles))
+        right.append(jnp.concatenate(one_hot(terms[1, r : r + 1, :], lane_ids), axis=0))
+    packed = dot_nt(jnp.concatenate(left, axis=1), jnp.concatenate(right, axis=1))
     for p in range(dev_count):
         lanes = slice(p // half_dev * LANES, (p // half_dev + 1) * LANES)
-        for c in range(5):
+        for c in range(CHANNELS):
             start = c * row_total + p % half_dev * per_dest
             rows = packed[start : start + per_dest, lanes]
             if c < 4:
-                start = (c + 5) * row_total + p % half_dev * per_dest
+                start = (c + CHANNELS) * row_total + p % half_dev * per_dest
                 rows = rows + packed[start : start + per_dest, lanes]
             send[p, c * per_dest : (c + 1) * per_dest, :] = rows
 
@@ -206,107 +207,81 @@
         data_copy(p, d).start()
         cost_copy(p, d).start()
 
-    late = dev_count - batch
-    for p in range(late):
+    for p in range(dev_count):
         when(p != d, lambda: send_to(p))
-    for p in range(late, dev_count):
-        when((own == BATCHES - 1) & (p != d), lambda: send_to(p))
     recv[d] = send[d]
 
-    def channels(x, j):
-        def channel(c):
-            rows = [
-                recv[x * batch + j * per_block + i, c * per_dest : (c + 1) * per_dest, :]
-                for i in range(per_block)
-            ]
-            return rows[0] if per_block == 1 else jnp.concatenate(rows, axis=0)
-
-        return [channel(c) for c in range(5)]
-
     elem_ids = sublane_ids(ELEM_DEV)
-    blocks = batch * capacity // CHUNK
-
-    def prepare(x):
-        for j in range(blocks):
-            u, v, w, forcing, owner = channels(x, j)
-            rows = slice(j * 8, j * 8 + 8)
-            second_w = basis_values(v)
-            weighted = [first * forcing for first in basis_values(u)]
-            for c, value in enumerate(basis_values(w)):
-                third[c, rows] = value
-            for i, (a, b) in enumerate(PAIRS):
-                outer[i, rows] = weighted[a] * second_w[b]
-            for h in range(8):
-                columns = slice((j * 8 + h) * LANES, (j * 8 + h + 1) * LANES)
-                onehot[:, columns] = one_hot(owner[h : h + 1, :], elem_ids)
-
-    face_count, inner_count = len(OUTER_PAIRS), len(INNER_PAIRS)
-
-    def products(pairs, start):
-        count = pairs.stop - pairs.start
-        for h in range(blocks * 8):
-            columns = slice(h * LANES, (h + 1) * LANES)
-            value = outer[pairs, h : h + 1, :] * third[:, h, :][None]
-            value = value.reshape(count * 8, LANES)
-            rounded = value.astype(BF16)
-            product[start : start + count * 8, columns] = rounded
-            rest = (value - rounded.astype(F32)).astype(BF16)
-            product[start + count * 8 : start + count * 16, columns] = rest
-
-    def face_products():
-        products(slice(0, face_count), 0)
-
-    def inner_products():
-        products(slice(face_count, len(PAIRS)), face_count * 16)
-
-    def add_rows(sums, total, first):
-        count = sums.shape[0]
-        value = total[0:count] + total[count : 2 * count]
-        if first:
-            sums[...] = value
+    slot_ids = sublane_ids(SLOTS)
+
+    def scatter(x, fresh):
+        left, right = [], []
+        for r in range(batch * per_dest):
+            source = x * batch + r // per_dest
+
+            def row(c):
+                start = c * per_dest + r % per_dest
+                return recv[source, start : start + 1, :]
+
+            values = [halves(row(c)) for c in range(4)]
+            tiles = [high for high, _ in values] + [low for _, low in values]
+            left.append(spread(one_hot(row(5), slot_ids), tiles))
+            right.append(jnp.concatenate(one_hot(row(4), elem_ids), axis=0))
+        total = dot_nt(jnp.concatenate(left, axis=1), jnp.concatenate(right, axis=1))
+        if fresh:
+            grid[...] = total
         else:
-            sums[...] += value
-
-    def all_rows(x, first):
-        prepare(x)
-        face_products()
-        inner_products()
-        total = dot_nt(product[...], onehot[...])
-        add_rows(face_rows, total[0 : face_count * 16], first)
-        add_rows(inner_rows, total[face_count * 16 :], first)
+            grid[...] += total
 
     def arrive(source):
         data_copy(source, source).wait_recv()
 
     for i in range(batch):
         when(own * batch + i != d, lambda: arrive(own * batch + i))
-    all_rows(own, True)
-
-    for p in range(late, dev_count):
-        when(own != BATCHES - 1, lambda: send_to(p))
-
-    def from_batch(t):
+    scatter(own, True)
+
+    def from_batch(t, carry):
         x = t - 1 + (t > own).astype(jnp.int32)
         for i in range(batch):
             arrive(x * batch + i)
-        return x
-
-    def middle(t, carry):
-        all_rows(from_batch(t), False)
+        scatter(x, False)
         return carry
 
-    lax.fori_loop(1, BATCHES - 1, middle, 0)
-    prepare(from_batch(BATCHES - 1))
-    face_products()
-    total = dot_nt(product[0 : face_count * 16], onehot[...])
-    add_rows(face_rows, total, False)
-
-    def place(sums, pairs):
-        for i, (a, b) in enumerate(pairs):
-            start = a * 64 + b * 8
-            raw[start : start + 8, :] = sums[i * 8 : i * 8 + 8, :]
-
-    place(face_rows, OUTER_PAIRS)
+    lax.fori_loop(1, BATCHES, from_batch, 0)
+
+    for half in range(2):
+        lanes = slice(half * LANES, (half + 1) * LANES)
+
+        def field(c):
+            high = grid[c * SLOTS : (c + 1) * SLOTS, lanes]
+            return high + grid[(c + 4) * SLOTS : (c + 5) * SLOTS, lanes]
+
+        forcing = field(3)
+        for values, sink in zip(range(3), (first, second, third)):
+            for k, value in enumerate(basis_values(field(values))):
+                value = value * forcing if values == 0 else value
+                sink[half, k * SLOTS : (k + 1) * SLOTS, :] = value
+
+    def contract(pairs):
+        for half in range(2):
+            sums = [None] * len(pairs)
+            for s in range(SLOTS):
+                w = third[half, pl.ds(s, 8, stride=SLOTS), :]
+                u, vw = {}, {}
+                for a, b in pairs:
+                    if a not in u:
+                        row = first[half, a * SLOTS + s : a * SLOTS + s + 1, :]
+                        u[a] = jnp.broadcast_to(row, (8, LANES))
+                    if b not in vw:
+                        vw[b] = second[half, b * SLOTS + s : b * SLOTS + s + 1, :] * w
+                for i, (a, b) in enumerate(pairs):
+                    value = u[a] * vw[b]
+                    sums[i] = value if sums[i] is None else sums[i] + value
+            for (a, b), value in zip(pairs, sums):
+                start = a * 64 + b * 8
+                raw[start : start + 8, half * LANES : (half + 1) * LANES] = value
+
+    contract(OUTER_PAIRS)
 
     lane = lax.broadcasted_iota(jnp.int32, (1, LANES), 1)
     lower_half = lane < 64
@@ -369,10 +344,8 @@
     for j in range(1, grp_count):
         group_copy(j).start()
 
-    inner_products()
-    total = dot_nt(product[face_count * 16 :], onehot[...])
-    add_rows(inner_rows, total, False)
-    place(inner_rows, INNER_PAIRS)
+    contract([pair for pair in INNER_PAIRS if pair[1] < 4])
+    contract([pair for pair in INNER_PAIRS if pair[1] >= 4])
 
     for i in range(2):
         when(gets_a[i], lambda: face_copy(i).wait_recv())
@@ -456,14 +429,12 @@
     obs_rows = row_count // LANES
     capacity = 2 * row_count // dev_count
     per_dest = capacity // LANES
-    packed_rows = dev_count // 2 * per_dest
-    batch_obs = dev_count // BATCHES * capacity
     vmem = pl.BlockSpec(memory_space=pltpu.VMEM)
     dma = pltpu.SemaphoreType.DMA
     regular = pltpu.SemaphoreType.REGULAR
     rows = [
         x.reshape(obs_rows, LANES)
-        for x in (obs_resid, obs_weight, obs_dest, obs_send_slot, obs_elem)
+        for x in (obs_resid, obs_weight, obs_dest, obs_send_slot, obs_elem, obs_slot)
     ]
     field, cost = pl.pallas_call(
         functools.partial(kernel, dev_count, grp_count, capacity),
@@ -471,7 +442,7 @@
             pltpu.VMEM((ELEM_DEV, 512), F32),
             pltpu.VMEM((1, LANES), F32),
         ),
-        in_specs=[pl.BlockSpec(memory_space=pl.ANY)] * 6,
+        in_specs=[pl.BlockSpec(memory_space=pl.ANY)] * 7,
         out_specs=(vmem, vmem),
         scratch_shapes=[
             pltpu.VMEM((3, row_count), F32),
@@ -480,27 +451,24 @@
             pltpu.VMEM((obs_rows, LANES), jnp.int32),
             pltpu.VMEM((obs_rows, LANES), jnp.int32),
             pltpu.VMEM((obs_rows, LANES), jnp.int32),
+            pltpu.VMEM((obs_rows, LANES), jnp.int32),
             pltpu.VMEM((5, obs_rows, LANES), F32),
-            pltpu.VMEM((9 * packed_rows, row_count), BF16),
-            pltpu.VMEM((2 * LANES, row_count), BF16),
-            pltpu.VMEM((dev_count, 5 * per_dest, LANES), F32),
-            pltpu.VMEM((dev_count, 5 * per_dest, LANES), F32),
+            pltpu.VMEM((dev_count, CHANNELS * per_dest, LANES), F32),
+            pltpu.VMEM((dev_count, CHANNELS * per_dest, LANES), F32),
             pltpu.VMEM((1, LANES), F32),
             pltpu.VMEM((dev_count, 1, LANES), F32),
             pltpu.VMEM((1, LANES), F32),
             pltpu.VMEM((grp_count, 1, LANES), F32),
-            pltpu.VMEM((8, batch_obs // LANES, LANES), F32),
-            pltpu.VMEM((64, batch_obs // LANES, LANES), F32),
-            pltpu.VMEM((1024, batch_obs), BF16),
-            pltpu.VMEM((ELEM_DEV, batch_obs), BF16),
+            pltpu.VMEM((8 * SLOTS, ELEM_DEV), F32),
+            pltpu.VMEM((2, 8 * SLOTS, LANES), F32),
+            pltpu.VMEM((2, 8 * SLOTS, LANES), F32),
+            pltpu.VMEM((2, 8 * SLOTS, LANES), F32),
             pltpu.VMEM((512, ELEM_DEV), F32),
             pltpu.VMEM((2, 32, LANES), F32),
             pltpu.VMEM((2, 32, LANES), F32),
             pltpu.VMEM((2, 2, 8, LANES), F32),
             pltpu.VMEM((2, 2, 8, LANES), F32),
             pltpu.VMEM((2, 2, 8, LANES), F32),
-            pltpu.VMEM((len(OUTER_PAIRS) * 8, ELEM_DEV), F32),
-            pltpu.VMEM((len(INNER_PAIRS) * 8, ELEM_DEV), F32),
             dma((dev_count,)),
             dma((dev_count,)),
             dma((dev_count,)),
@@ -511,7 +479,7 @@
             dma((4,)),
             dma((2, 2)),
             dma((2, 2)),
-            dma((6,)),
+            dma((7,)),
             regular((dev_count,)),
             regular,
         ],

time: 21.9 us -> 20.3 us (0.927)
  the two profiles are of different devices: /device:TPU:19 before, /device:TPU:1 now
where the time goes in v2:
time: 20.3 us; the launch traced here: 20 us
  Pallas kernels  17.4 us (86%)
  between operations  1.81 us (9%)
  local copies, waits for them, and re-layouts  0.8 us (4%)
    pallas_call x1, Pallas kernels, on_device(): pl.pallas_call(functools.partial(kernel, dev_count, grp_count, capacity),...  17.4 us
    unnamed x1, local copies, waits for them, and re-layouts  0.8 us

profile of v2, /device:TPU:1, one launch (start us, length us, event | category | flops | bytes accessed | tf_op | source)
XLA Modules:
  0.0 20.0 jit_solution(6297091414982208019)
XLA Ops:
  0.6 17.4 %shard_map.86 = (f32[256,512]{1,0:T(8,128)S(1)}, f32[1,128]{1,0:T(1,128)S(1)}) custom-call(f32[3,4096]{1,0:T(4,128)} %coord_in.1, f32[32,128]{1,0:T(8,128)} %bitcast.11, f32[32,128]{1,0:T(8,128)} %bitcast.12, s32[32,128]{1,0:T(8,128)} %bitcast.13, s32[32,128]{1,0:T(8,128)} %bitcast.14, s32[32,128]{1,0:T(8,128)} %bitcast.15, s32[32,128]{1,0:T(8,128)} %bitcast.16), custom_call_target="tpu_custom_call" | custom-call | tf_op jit(solution)/shard_map/pallas_call | solution.py:439
  18.1 0.8 %copy.11 = f32[4,8,8,512]{3,2,1,0:T(8,128)} copy(f32[4,8,8,512]{3,2,1,0:T(8,128)S(1)} %bitcast.9) | data formatting | bytes 1048576

commit v3 on v2

--- a/solution.py
+++ b/solution.py
@@ -13,8 +13,7 @@
 EZ = 8
 ELEM_DEV = 256
 LANES = 128
-SLOTS = 32
-CHANNELS = 6
+CHANNELS = 5
 BATCHES = 4
 MESH = pl.DeviceIdType.MESH
 F32 = jnp.float32
@@ -76,11 +75,11 @@
 
 def kernel(
     dev_count, grp_count, capacity,
-    coord_in, resid_in, weight_in, dest_in, send_slot_in, elem_in, slot_in,
+    coord_in, resid_in, weight_in, dest_in, slot_in, elem_in,
     out, cost,
-    coord, resid, weight, dest, send_slot, elem, slot, terms, send, recv,
+    coord, resid, weight, dest, slot, elem, terms, send, recv,
     cost_send, cost_recv, group_send, group_recv,
-    grid, first, second, third, raw, a_send, a_recv, b_send, b_recv, edge_recv,
+    outer, third, face_rows, inner_rows, raw, a_send, a_recv, b_send, b_recv, edge_recv,
     send_sem, recv_sem, cost_send_sem, cost_recv_sem, group_send_sem, group_recv_sem,
     face_send_sem, face_recv_sem, edge_send_sem, edge_recv_sem, load_sem,
     up_sem, others_sem,
@@ -108,8 +107,8 @@
         pltpu.make_async_copy(source, sink, load_sem.at[i])
         for i, (source, sink) in enumerate(
             zip(
-                (dest_in, send_slot_in, resid_in, weight_in, coord_in, elem_in, slot_in),
-                (dest, send_slot, resid, weight, coord, elem, slot),
+                (dest_in, slot_in, resid_in, weight_in, coord_in, elem_in),
+                (dest, slot, resid, weight, coord, elem),
             )
         )
     ]
@@ -147,37 +146,48 @@
     residual = resid[...]
     forcing = weight[...] * residual
     where = dest[...]
-    which = send_slot[...]
+    which = slot[...]
     terms[0] = ((where % half_dev) * per_dest + which // LANES).astype(F32)
     terms[1] = ((where // half_dev) * LANES + which % LANES).astype(F32)
     terms[2] = forcing
     terms[3] = elem[...].astype(F32)
-    terms[4] = slot[...].astype(F32)
     part = jnp.sum(forcing * residual, axis=0, keepdims=True)
     cost_send[...] = jnp.broadcast_to(0.5 * jnp.sum(part, axis=1, keepdims=True), (1, LANES))
 
     row_ids = sublane_ids(row_total)
     lane_ids = sublane_ids(2 * LANES)
-    left, right = [], []
-    for r in range(obs_rows):
-        columns = slice(r * LANES, (r + 1) * LANES)
-        values = [halves(coord[c : c + 1, columns]) for c in range(3)]
-        values.append(halves(terms[2, r : r + 1, :]))
-        tiles = [high for high, _ in values]
-        tiles += [halves(terms[i, r : r + 1, :])[0] for i in (3, 4)]
-        tiles += [low for _, low in values]
-        left.append(spread(one_hot(terms[0, r : r + 1, :], row_ids), tiles))
-        right.append(jnp.concatenate(one_hot(terms[1, r : r + 1, :], lane_ids), axis=0))
-    packed = dot_nt(jnp.concatenate(left, axis=1), jnp.concatenate(right, axis=1))
-    for p in range(dev_count):
-        lanes = slice(p // half_dev * LANES, (p // half_dev + 1) * LANES)
-        for c in range(CHANNELS):
-            start = c * row_total + p % half_dev * per_dest
-            rows = packed[start : start + per_dest, lanes]
-            if c < 4:
-                start = (c + CHANNELS) * row_total + p % half_dev * per_dest
-                rows = rows + packed[start : start + per_dest, lanes]
-            send[p, c * per_dest : (c + 1) * per_dest, :] = rows
+    once = jnp.minimum(d + 1, 1)
+
+    def looped(body):
+        def step(_, carry):
+            body()
+            return carry
+
+        lax.fori_loop(0, once, step, 0)
+
+    def pack():
+        left, right = [], []
+        for r in range(obs_rows):
+            columns = slice(r * LANES, (r + 1) * LANES)
+            values = [halves(coord[c : c + 1, columns]) for c in range(3)]
+            values.append(halves(terms[2, r : r + 1, :]))
+            tiles = [high for high, _ in values]
+            tiles.append(halves(terms[3, r : r + 1, :])[0])
+            tiles += [low for _, low in values]
+            left.append(spread(one_hot(terms[0, r : r + 1, :], row_ids), tiles))
+            right.append(jnp.concatenate(one_hot(terms[1, r : r + 1, :], lane_ids), axis=0))
+        packed = dot_nt(jnp.concatenate(left, axis=1), jnp.concatenate(right, axis=1))
+        for p in range(dev_count):
+            lanes = slice(p // half_dev * LANES, (p // half_dev + 1) * LANES)
+            for c in range(CHANNELS):
+                start = c * row_total + p % half_dev * per_dest
+                rows = packed[start : start + per_dest, lanes]
+                if c < 4:
+                    start = (c + CHANNELS) * row_total + p % half_dev * per_dest
+                    rows = rows + packed[start : start + per_dest, lanes]
+                send[p, c * per_dest : (c + 1) * per_dest, :] = rows
+
+    looped(pack)
 
     def data_copy(p, source):
         return pltpu.make_async_remote_copy(
@@ -207,81 +217,93 @@
         data_copy(p, d).start()
         cost_copy(p, d).start()
 
-    for p in range(dev_count):
+    late = dev_count - batch
+    for p in range(late):
         when(p != d, lambda: send_to(p))
+    for p in range(late, dev_count):
+        when((own >= BATCHES - 2) & (p != d), lambda: send_to(p))
     recv[d] = send[d]
 
     elem_ids = sublane_ids(ELEM_DEV)
-    slot_ids = sublane_ids(SLOTS)
-
-    def scatter(x, fresh):
+    rows = batch * per_dest
+
+    def prepare(x):
+        def channel(c):
+            start = c * per_dest
+            parts = [recv[x * batch + i, start : start + per_dest, :] for i in range(batch)]
+            return jnp.concatenate(parts, axis=0)
+
+        weighted = [first * channel(3) for first in basis_values(channel(0))]
+        second = basis_values(channel(1))
+        for c, value in enumerate(basis_values(channel(2))):
+            third[c * rows : (c + 1) * rows, :] = value
+        for i, (a, b) in enumerate(PAIRS):
+            outer[i] = weighted[a] * second[b]
+
+    def pair_sums(x, groups):
         left, right = [], []
-        for r in range(batch * per_dest):
-            source = x * batch + r // per_dest
-
-            def row(c):
-                start = c * per_dest + r % per_dest
-                return recv[source, start : start + 1, :]
-
-            values = [halves(row(c)) for c in range(4)]
-            tiles = [high for high, _ in values] + [low for _, low in values]
-            left.append(spread(one_hot(row(5), slot_ids), tiles))
-            right.append(jnp.concatenate(one_hot(row(4), elem_ids), axis=0))
+        for h in range(rows):
+            w = third[pl.ds(h, 8, stride=rows), :]
+            pieces = []
+            for start, stop in groups:
+                highs, lows = [], []
+                for i in range(start, stop, 2):
+                    value = jnp.concatenate([outer[k, h : h + 1, :] * w for k in (i, i + 1)], axis=0)
+                    high = value.astype(BF16)
+                    highs.append(high)
+                    lows.append((value - high.astype(F32)).astype(BF16))
+                pieces += highs + lows
+            left.append(jnp.concatenate(pieces, axis=0))
+            start = 4 * per_dest + h % per_dest
+            owner = recv[x * batch + h // per_dest, start : start + 1, :]
+            right.append(jnp.concatenate(one_hot(owner, elem_ids), axis=0))
         total = dot_nt(jnp.concatenate(left, axis=1), jnp.concatenate(right, axis=1))
-        if fresh:
-            grid[...] = total
-        else:
-            grid[...] += total
+        sums, row = [], 0
+        for start, stop in groups:
+            count = (stop - start) * 8
+            sums.append(total[row : row + count] + total[row + count : row + 2 * count])
+            row += 2 * count
+        return sums
+
+    faces, inners = (0, len(OUTER_PAIRS)), (len(OUTER_PAIRS), len(PAIRS))
 
     def arrive(source):
         data_copy(source, source).wait_recv()
 
     for i in range(batch):
         when(own * batch + i != d, lambda: arrive(own * batch + i))
-    scatter(own, True)
-
-    def from_batch(t, carry):
+
+    def first_sums():
+        prepare(own)
+        face_rows[...], inner_rows[...] = pair_sums(own, (faces, inners))
+
+    looped(first_sums)
+
+    for p in range(late, dev_count):
+        when(own < BATCHES - 2, lambda: send_to(p))
+
+    def from_batch(t):
         x = t - 1 + (t > own).astype(jnp.int32)
         for i in range(batch):
             arrive(x * batch + i)
-        scatter(x, False)
+        prepare(x)
+        return x
+
+    def middle(t, carry):
+        face, inner = pair_sums(from_batch(t), (faces, inners))
+        face_rows[...] += face
+        inner_rows[...] += inner
         return carry
 
-    lax.fori_loop(1, BATCHES, from_batch, 0)
-
-    for half in range(2):
-        lanes = slice(half * LANES, (half + 1) * LANES)
-
-        def field(c):
-            high = grid[c * SLOTS : (c + 1) * SLOTS, lanes]
-            return high + grid[(c + 4) * SLOTS : (c + 5) * SLOTS, lanes]
-
-        forcing = field(3)
-        for values, sink in zip(range(3), (first, second, third)):
-            for k, value in enumerate(basis_values(field(values))):
-                value = value * forcing if values == 0 else value
-                sink[half, k * SLOTS : (k + 1) * SLOTS, :] = value
-
-    def contract(pairs):
-        for half in range(2):
-            sums = [None] * len(pairs)
-            for s in range(SLOTS):
-                w = third[half, pl.ds(s, 8, stride=SLOTS), :]
-                u, vw = {}, {}
-                for a, b in pairs:
-                    if a not in u:
-                        row = first[half, a * SLOTS + s : a * SLOTS + s + 1, :]
-                        u[a] = jnp.broadcast_to(row, (8, LANES))
-                    if b not in vw:
-                        vw[b] = second[half, b * SLOTS + s : b * SLOTS + s + 1, :] * w
-                for i, (a, b) in enumerate(pairs):
-                    value = u[a] * vw[b]
-                    sums[i] = value if sums[i] is None else sums[i] + value
-            for (a, b), value in zip(pairs, sums):
-                start = a * 64 + b * 8
-                raw[start : start + 8, half * LANES : (half + 1) * LANES] = value
-
-    contract(OUTER_PAIRS)
+    lax.fori_loop(1, BATCHES - 1, middle, 0)
+    last = from_batch(BATCHES - 1)
+
+    def place(value, pairs):
+        for i, (a, b) in enumerate(pairs):
+            start = a * 64 + b * 8
+            raw[start : start + 8, :] = value[i * 8 : i * 8 + 8]
+
+    looped(lambda: place(face_rows[...] + pair_sums(last, (faces,))[0], OUTER_PAIRS))
 
     lane = lax.broadcasted_iota(jnp.int32, (1, LANES), 1)
     lower_half = lane < 64
@@ -344,8 +366,7 @@
     for j in range(1, grp_count):
         group_copy(j).start()
 
-    contract([pair for pair in INNER_PAIRS if pair[1] < 4])
-    contract([pair for pair in INNER_PAIRS if pair[1] >= 4])
+    looped(lambda: place(inner_rows[...] + pair_sums(last, (inners,))[0], INNER_PAIRS))
 
     for i in range(2):
         when(gets_a[i], lambda: face_copy(i).wait_recv())
@@ -429,12 +450,13 @@
     obs_rows = row_count // LANES
     capacity = 2 * row_count // dev_count
     per_dest = capacity // LANES
+    batch_rows = dev_count // BATCHES * per_dest
     vmem = pl.BlockSpec(memory_space=pltpu.VMEM)
     dma = pltpu.SemaphoreType.DMA
     regular = pltpu.SemaphoreType.REGULAR
     rows = [
         x.reshape(obs_rows, LANES)
-        for x in (obs_resid, obs_weight, obs_dest, obs_send_slot, obs_elem, obs_slot)
+        for x in (obs_resid, obs_weight, obs_dest, obs_send_slot, obs_elem)
     ]
     field, cost = pl.pallas_call(
         functools.partial(kernel, dev_count, grp_count, capacity),
@@ -442,7 +464,7 @@
             pltpu.VMEM((ELEM_DEV, 512), F32),
             pltpu.VMEM((1, LANES), F32),
         ),
-        in_specs=[pl.BlockSpec(memory_space=pl.ANY)] * 7,
+        in_specs=[pl.BlockSpec(memory_space=pl.ANY)] * 6,
         out_specs=(vmem, vmem),
         scratch_shapes=[
             pltpu.VMEM((3, row_count), F32),
@@ -451,18 +473,17 @@
             pltpu.VMEM((obs_rows, LANES), jnp.int32),
             pltpu.VMEM((obs_rows, LANES), jnp.int32),
             pltpu.VMEM((obs_rows, LANES), jnp.int32),
-            pltpu.VMEM((obs_rows, LANES), jnp.int32),
-            pltpu.VMEM((5, obs_rows, LANES), F32),
+            pltpu.VMEM((4, obs_rows, LANES), F32),
             pltpu.VMEM((dev_count, CHANNELS * per_dest, LANES), F32),
             pltpu.VMEM((dev_count, CHANNELS * per_dest, LANES), F32),
             pltpu.VMEM((1, LANES), F32),
             pltpu.VMEM((dev_count, 1, LANES), F32),
             pltpu.VMEM((1, LANES), F32),
             pltpu.VMEM((grp_count, 1, LANES), F32),
-            pltpu.VMEM((8 * SLOTS, ELEM_DEV), F32),
-            pltpu.VMEM((2, 8 * SLOTS, LANES), F32),
-            pltpu.VMEM((2, 8 * SLOTS, LANES), F32),
-            pltpu.VMEM((2, 8 * SLOTS, LANES), F32),
+            pltpu.VMEM((64, batch_rows, LANES), F32),
+            pltpu.VMEM((8 * batch_rows, LANES), F32),
+            pltpu.VMEM((len(OUTER_PAIRS) * 8, ELEM_DEV), F32),
+            pltpu.VMEM((len(INNER_PAIRS) * 8, ELEM_DEV), F32),
             pltpu.VMEM((512, ELEM_DEV), F32),
             pltpu.VMEM((2, 32, LANES), F32),
             pltpu.VMEM((2, 32, LANES), F32),
@@ -479,7 +500,7 @@
             dma((4,)),
             dma((2, 2)),
             dma((2, 2)),
-            dma((7,)),
+            dma((6,)),
             regular((dev_count,)),
             regular,
         ],

time: 20.3 us -> 19.7 us (0.970)
  Pallas kernels: 17.4 us -> 16.8 us
    pallas_call x1, Pallas kernels: 17.4 us -> 16.8 us  [on_device(): pl.pallas_call(functools.partial(kernel, dev_count, grp_count, capacity),...]
where the time goes in v3:
time: 19.7 us; the launch traced here: 19.4 us
  Pallas kernels  16.8 us (85%)
  between operations  1.8 us (9%)
  local copies, waits for them, and re-layouts  0.8 us (4%)
    pallas_call x1, Pallas kernels, on_device(): pl.pallas_call(functools.partial(kernel, dev_count, grp_count, capacity),...  16.8 us
    unnamed x1, local copies, waits for them, and re-layouts  0.8 us

profile of v3, /device:TPU:1, one launch (start us, length us, event | category | flops | bytes accessed | tf_op | source)
XLA Modules:
  0.0 19.4 jit_solution(5753922238096235703)
XLA Ops:
  0.6 16.8 %shard_map.77 = (f32[256,512]{1,0:T(8,128)S(1)}, f32[1,128]{1,0:T(1,128)S(1)}) custom-call(f32[3,4096]{1,0:T(4,128)} %coord_in.1, f32[32,128]{1,0:T(8,128)} %bitcast.10, f32[32,128]{1,0:T(8,128)} %bitcast.11, s32[32,128]{1,0:T(8,128)} %bitcast.12, s32[32,128]{1,0:T(8,128)} %bitcast.13, s32[32,128]{1,0:T(8,128)} %bitcast.14), custom_call_target="tpu_custom_call" | custom-call | tf_op jit(solution)/shard_map/pallas_call | solution.py:461
  17.4 0.8 %copy.10 = f32[4,8,8,512]{3,2,1,0:T(8,128)} copy(f32[4,8,8,512]{3,2,1,0:T(8,128)S(1)} %bitcast.8) | data formatting | bytes 1048576

commit v4 on v3

--- a/solution.py
+++ b/solution.py
@@ -18,6 +18,7 @@
 MESH = pl.DeviceIdType.MESH
 F32 = jnp.float32
 BF16 = jnp.bfloat16
+F8 = jnp.float8_e4m3fn
 
 ANCHORS = [-math.cos(math.pi * k / 7) for k in range(8)]
 OUTER_PAIRS = [(a, b) for a in (0, 7) for b in range(8)]
@@ -60,7 +61,7 @@
 
 
 def one_hot(row, ids):
-    tile = jnp.broadcast_to(row, (16, LANES)).astype(BF16)
+    tile = jnp.broadcast_to(row, (ids[0].shape[0], LANES)).astype(BF16)
     return [jnp.where(part == tile, jnp.ones((), BF16), jnp.zeros((), BF16)) for part in ids]
 
 
@@ -68,9 +69,9 @@
     return jnp.concatenate([part * tile for tile in tiles for part in hot], axis=0)
 
 
-def sublane_ids(count):
-    ids = lax.broadcasted_iota(jnp.int32, (16, LANES), 0)
-    return [(ids + 16 * i).astype(F32).astype(BF16) for i in range(count // 16)]
+def sublane_ids(count, step=16):
+    ids = lax.broadcasted_iota(jnp.int32, (step, LANES), 0)
+    return [(ids + step * i).astype(F32).astype(BF16) for i in range(count // step)]
 
 
 def kernel(
@@ -78,9 +79,9 @@
     coord_in, resid_in, weight_in, dest_in, slot_in, elem_in,
     out, cost,
     coord, resid, weight, dest, slot, elem, terms, send, recv,
-    cost_send, cost_recv, group_send, group_recv,
+    group_send, group_recv,
     outer, third, face_rows, inner_rows, raw, a_send, a_recv, b_send, b_recv, edge_recv,
-    send_sem, recv_sem, cost_send_sem, cost_recv_sem, group_send_sem, group_recv_sem,
+    send_sem, recv_sem, group_send_sem, group_recv_sem,
     face_send_sem, face_recv_sem, edge_send_sem, edge_recv_sem, load_sem,
     up_sem, others_sem,
 ):
@@ -89,7 +90,8 @@
     obs_rows = resid.shape[0]
     per_dest = capacity // LANES
     half_dev = dev_count // 2
-    row_total = half_dev * per_dest
+    quarter_dev = half_dev // 2
+    row_total = quarter_dev * per_dest
     batch = dev_count // BATCHES
 
     def when(condition, action):
@@ -134,12 +136,6 @@
         when(jnp.logical_not(lower), lambda: signal(barrier, partner))
         lower_count = lower_count + lower.astype(jnp.int32)
         higher_others = higher_others - lower.astype(jnp.int32)
-    when(lower_count > 0, lambda: pl.semaphore_wait(barrier, lower_count))
-    for p in range(dev_count):
-        when(p < d, lambda: signal(up_sem.at[d], (g, p)))
-    for partner in others:
-        when(is_lower(partner), lambda: signal(others_sem, partner))
-
     for load in loads:
         load.wait()
 
@@ -147,15 +143,20 @@
     forcing = weight[...] * residual
     where = dest[...]
     which = slot[...]
-    terms[0] = ((where % half_dev) * per_dest + which // LANES).astype(F32)
-    terms[1] = ((where // half_dev) * LANES + which % LANES).astype(F32)
-    terms[2] = forcing
-    terms[3] = elem[...].astype(F32)
+    row = where % quarter_dev * per_dest + which // LANES
+    for half in range(2):
+        terms[half] = jnp.where(where // half_dev == half, row, -1).astype(F32)
+    terms[2] = (where // quarter_dev % 2 * LANES + which % LANES).astype(F32)
+    terms[3] = forcing
+    terms[4] = elem[...].astype(F32)
     part = jnp.sum(forcing * residual, axis=0, keepdims=True)
-    cost_send[...] = jnp.broadcast_to(0.5 * jnp.sum(part, axis=1, keepdims=True), (1, LANES))
+    part = jnp.broadcast_to(0.5 * jnp.sum(part, axis=1, keepdims=True), (1, LANES))
+    cost_row = slice(CHANNELS * per_dest, CHANNELS * per_dest + 1)
+    for p in range(dev_count):
+        send[p, cost_row, :] = part
 
     row_ids = sublane_ids(row_total)
-    lane_ids = sublane_ids(2 * LANES)
+    lane_ids = sublane_ids(2 * LANES, 32)
     once = jnp.minimum(d + 1, 1)
 
     def looped(body):
@@ -165,29 +166,28 @@
 
         lax.fori_loop(0, once, step, 0)
 
-    def pack():
+    def pack(half):
         left, right = [], []
         for r in range(obs_rows):
             columns = slice(r * LANES, (r + 1) * LANES)
             values = [halves(coord[c : c + 1, columns]) for c in range(3)]
-            values.append(halves(terms[2, r : r + 1, :]))
+            values.append(halves(terms[3, r : r + 1, :]))
             tiles = [high for high, _ in values]
-            tiles.append(halves(terms[3, r : r + 1, :])[0])
+            tiles.append(halves(terms[4, r : r + 1, :])[0])
             tiles += [low for _, low in values]
-            left.append(spread(one_hot(terms[0, r : r + 1, :], row_ids), tiles))
-            right.append(jnp.concatenate(one_hot(terms[1, r : r + 1, :], lane_ids), axis=0))
+            left.append(spread(one_hot(terms[half, r : r + 1, :], row_ids), tiles))
+            hot = one_hot(terms[2, r : r + 1, :], lane_ids)
+            right.append(jnp.concatenate([part.astype(F8) for part in hot], axis=0))
         packed = dot_nt(jnp.concatenate(left, axis=1), jnp.concatenate(right, axis=1))
-        for p in range(dev_count):
-            lanes = slice(p // half_dev * LANES, (p // half_dev + 1) * LANES)
+        for q in range(half_dev):
+            lanes = slice(q // quarter_dev * LANES, (q // quarter_dev + 1) * LANES)
             for c in range(CHANNELS):
-                start = c * row_total + p % half_dev * per_dest
+                start = c * row_total + q % quarter_dev * per_dest
                 rows = packed[start : start + per_dest, lanes]
                 if c < 4:
-                    start = (c + CHANNELS) * row_total + p % half_dev * per_dest
+                    start = (c + CHANNELS) * row_total + q % quarter_dev * per_dest
                     rows = rows + packed[start : start + per_dest, lanes]
-                send[p, c * per_dest : (c + 1) * per_dest, :] = rows
-
-    looped(pack)
+                send[half * half_dev + q, c * per_dest : (c + 1) * per_dest, :] = rows
 
     def data_copy(p, source):
         return pltpu.make_async_remote_copy(
@@ -196,13 +196,6 @@
             device_id=(g, p), device_id_type=MESH,
         )
 
-    def cost_copy(p, source):
-        return pltpu.make_async_remote_copy(
-            src_ref=cost_send, dst_ref=cost_recv.at[source],
-            send_sem=cost_send_sem.at[p], recv_sem=cost_recv_sem.at[source],
-            device_id=(g, p), device_id_type=MESH,
-        )
-
     def group_copy(j):
         return pltpu.make_async_remote_copy(
             src_ref=group_send, dst_ref=group_recv.at[j],
@@ -215,13 +208,21 @@
     def send_to(p):
         when(p > d, lambda: pl.semaphore_wait(up_sem.at[p], 1))
         data_copy(p, d).start()
-        cost_copy(p, d).start()
-
-    late = dev_count - batch
-    for p in range(late):
-        when(p != d, lambda: send_to(p))
-    for p in range(late, dev_count):
-        when((own >= BATCHES - 2) & (p != d), lambda: send_to(p))
+
+    looped(lambda: pack(0))
+    when(lower_count > 0, lambda: pl.semaphore_wait(barrier, lower_count))
+    for p in range(dev_count):
+        when(p < d, lambda: signal(up_sem.at[d], (g, p)))
+    for partner in others:
+        when(is_lower(partner), lambda: signal(others_sem, partner))
+
+    for p in range(half_dev):
+        when(p < d, lambda: send_to(p))
+    looped(lambda: pack(1))
+    for p in range(half_dev, dev_count):
+        when(p < d, lambda: send_to(p))
+    for i in range(batch):
+        when(own * batch + i > d, lambda: send_to(own * batch + i))
     recv[d] = send[d]
 
     elem_ids = sublane_ids(ELEM_DEV)
@@ -279,17 +280,26 @@
 
     looped(first_sums)
 
-    for p in range(late, dev_count):
-        when(own < BATCHES - 2, lambda: send_to(p))
+    def send_up(x):
+        for i in range(batch):
+            when(x < BATCHES, lambda: send_to(x * batch + i))
+
+    send_up(own + 1)
+    send_up(own + 2)
 
     def from_batch(t):
-        x = t - 1 + (t > own).astype(jnp.int32)
+        early = own < BATCHES // 2
+        turn = jnp.where(early, own, BATCHES - 1 - own)
+        x = t - 1 + (t > turn).astype(jnp.int32)
+        x = jnp.where(early, x, BATCHES - 1 - x)
         for i in range(batch):
             arrive(x * batch + i)
         prepare(x)
         return x
 
     def middle(t, carry):
+        for j in range(3, BATCHES):
+            when(t == j - 1, lambda: send_up(own + j))
         face, inner = pair_sums(from_batch(t), (faces, inners))
         face_rows[...] += face
         inner_rows[...] += inner
@@ -297,28 +307,36 @@
 
     lax.fori_loop(1, BATCHES - 1, middle, 0)
     last = from_batch(BATCHES - 1)
+    when(higher_others > 0, lambda: pl.semaphore_wait(others_sem, higher_others))
+    group_cost = recv[0, cost_row, :]
+    for i in range(1, dev_count):
+        group_cost = group_cost + recv[i, cost_row, :]
+    group_send[...] = group_cost
+    for j in range(1, grp_count):
+        group_copy(j).start()
 
     def place(value, pairs):
         for i, (a, b) in enumerate(pairs):
             start = a * 64 + b * 8
-            raw[start : start + 8, :] = value[i * 8 : i * 8 + 8]
+            for half in range(2):
+                lanes = slice(half * LANES, (half + 1) * LANES)
+                raw[half, start : start + 8, :] = value[i * 8 : i * 8 + 8, lanes]
 
     looped(lambda: place(face_rows[...] + pair_sums(last, (faces,))[0], OUTER_PAIRS))
 
     lane = lax.broadcasted_iota(jnp.int32, (1, LANES), 1)
     lower_half = lane < 64
     node = (lane // 8) % 8
-    block = raw[448:512, 128:256]
+    block = raw[1, 448:512, :]
     a_send[0] = jnp.where(lower_half, pltpu.roll(block[0:32], 64, 1), block[32:64])
-    block = raw[0:64, 0:128]
+    block = raw[0, 0:64, :]
     a_send[1] = jnp.where(lower_half, block[0:32], pltpu.roll(block[32:64], 64, 1))
     for half in range(2):
-        columns = slice(half * LANES, (half + 1) * LANES)
-        up = pltpu.roll(raw[56:64, columns], 72, 1)
-        down = raw[0:8, columns]
+        up = pltpu.roll(raw[half, 56:64, :], 72, 1)
+        down = raw[half, 0:8, :]
         for a in range(1, 8):
-            high = raw[a * 64 + 56 : a * 64 + 64, columns]
-            low = raw[a * 64 : a * 64 + 8, columns]
+            high = raw[half, a * 64 + 56 : a * 64 + 64, :]
+            low = raw[half, a * 64 : a * 64 + 8, :]
             up = jnp.where(node == a, pltpu.roll(high, (a * 8 + 72) % 128, 1), up)
             down = jnp.where(node == a, pltpu.roll(low, a * 8, 1), down)
         b_send[0, half] = up
@@ -350,7 +368,6 @@
     def clear(ref, i):
         ref[i] = jnp.zeros_like(ref[i])
 
-    when(higher_others > 0, lambda: pl.semaphore_wait(others_sem, higher_others))
     for j in range(2):
         for i in range(2):
             when(sends_a[i] & sends_b[j], lambda: edge_copy(i, j).start())
@@ -358,29 +375,45 @@
         when(sends_a[i], lambda: face_copy(i).start())
         when(sends_b[i], lambda: face_copy(2 + i).start())
 
-    group_cost = cost_send[...]
-    for i in range(dev_count):
-        when(i != d, lambda: cost_copy(i, i).wait_recv())
-        group_cost = group_cost + jnp.where(i == d, 0.0, cost_recv[i])
-    group_send[...] = group_cost
-    for j in range(1, grp_count):
-        group_copy(j).start()
-
     looped(lambda: place(inner_rows[...] + pair_sums(last, (inners,))[0], INNER_PAIRS))
+
+    low_rows, high_rows = slice(0, 64), slice(448, 512)
+    low = [raw[half, low_rows, :] for half in range(2)]
+    high = [raw[half, high_rows, :] for half in range(2)]
+    low_rolled = [pltpu.roll(x, 64, 1) for x in low]
+    high_rolled = [pltpu.roll(x, 64, 1) for x in high]
+    raw[0, low_rows, :] = low[0] + jnp.where(lower_half, 0.0, high_rolled[0])
+    raw[1, low_rows, :] = low[1] + jnp.where(lower_half, high_rolled[0], high_rolled[1])
+    raw[0, high_rows, :] = high[0] + jnp.where(lower_half, low_rolled[0], low_rolled[1])
+    raw[1, high_rows, :] = high[1] + jnp.where(lower_half, low_rolled[1], 0.0)
+
+    def from_below(high):
+        return jnp.where(node == 0, 0.0, pltpu.roll(high, 8, 1))
+
+    def from_above(low):
+        return jnp.where(node == 7, 0.0, pltpu.roll(low, 120, 1))
+
+    for half in range(2):
+        for a in range(8):
+            low_rows, high_rows = slice(a * 64, a * 64 + 8), slice(a * 64 + 56, a * 64 + 64)
+            low, high = raw[half, low_rows, :], raw[half, high_rows, :]
+            raw[half, low_rows, :] = low + from_below(high)
+            raw[half, high_rows, :] = high + from_above(low)
 
     for i in range(2):
         when(gets_a[i], lambda: face_copy(i).wait_recv())
         when(jnp.logical_not(gets_a[i]), lambda: clear(a_recv, i))
-    low, high = raw[0:64, :], raw[448:512, :]
-    from_low, from_high = a_recv[0], a_recv[1]
-    from_low = jnp.concatenate([from_low, pltpu.roll(from_low, 64, 1)], axis=0)
-    from_high = jnp.concatenate([pltpu.roll(from_high, 64, 1), from_high], axis=0)
-    high_rolled = [pltpu.roll(high[:, :128], 64, 1), pltpu.roll(high[:, 128:], 64, 1)]
-    low_rolled = [pltpu.roll(low[:, :128], 64, 1), pltpu.roll(low[:, 128:], 64, 1)]
-    raw[0:64, 0:128] = low[:, :128] + jnp.where(lower_half, from_low, high_rolled[0])
-    raw[0:64, 128:256] = low[:, 128:] + jnp.where(lower_half, high_rolled[0], high_rolled[1])
-    raw[448:512, 0:128] = high[:, :128] + jnp.where(lower_half, low_rolled[0], low_rolled[1])
-    raw[448:512, 128:256] = high[:, 128:] + jnp.where(lower_half, low_rolled[1], from_high)
+    for i in range(2):
+        got = a_recv[i]
+        parts = [got, pltpu.roll(got, 64, 1)]
+        if i == 0:
+            got = jnp.where(lower_half, jnp.concatenate(parts, axis=0), 0.0)
+        else:
+            got = jnp.where(lower_half, 0.0, jnp.concatenate(parts[::-1], axis=0))
+        start = i * 448
+        raw[i, start : start + 8, :] += got[0:8] + from_below(got[56:64])
+        raw[i, start + 8 : start + 56, :] += got[8:56]
+        raw[i, start + 56 : start + 64, :] += got[56:64] + from_above(got[0:8])
 
     faces = []
     for j in range(2):
@@ -402,28 +435,24 @@
             )
         faces.append(face)
     for half in range(2):
-        columns = slice(half * LANES, (half + 1) * LANES)
         for a in range(8):
-            low_rows = slice(a * 64, a * 64 + 8)
-            high_rows = slice(a * 64 + 56, a * 64 + 64)
-            low, high = raw[low_rows, columns], raw[high_rows, columns]
+            low_rows, high_rows = slice(a * 64, a * 64 + 8), slice(a * 64 + 56, a * 64 + 64)
             got_low = pltpu.roll(faces[0][half], (128 - a * 8) % 128, 1)
             got_high = pltpu.roll(faces[1][half], (56 - a * 8) % 128, 1)
-            raw[low_rows, columns] = low + jnp.where(node == 0, got_low, pltpu.roll(high, 8, 1))
-            raw[high_rows, columns] = high + jnp.where(node == 7, got_high, pltpu.roll(low, 120, 1))
-
-    ez = lax.broadcasted_iota(jnp.int32, (1, 8, LANES), 2) % 8
-    c = lax.broadcasted_iota(jnp.int32, (1, 8, LANES), 1)
-    takes_low = (c == 0) & (ez > 0)
-    takes_high = (c == 7) & (ez < 7)
+            raw[half, low_rows, :] += jnp.where(node == 0, got_low, 0.0)
+            raw[half, high_rows, :] += jnp.where(node == 7, got_high, 0.0)
+
+    ez = lane % 8
     for half in range(2):
+        for a in range(8):
+            low_rows = pl.ds(a * 64, 8, stride=8)
+            high_rows = pl.ds(a * 64 + 7, 8, stride=8)
+            low, high = raw[half, low_rows, :], raw[half, high_rows, :]
+            raw[half, low_rows, :] = low + jnp.where(ez > 0, pltpu.roll(high, 1, 1), 0.0)
+            raw[half, high_rows, :] = high + jnp.where(ez < 7, pltpu.roll(low, 127, 1), 0.0)
         for part in range(4):
             rows = slice(part * 128, (part + 1) * 128)
-            field = raw[rows, half * LANES : (half + 1) * LANES].reshape(16, 8, LANES)
-            below = pltpu.roll(pltpu.roll(field, 1, 2), 1, 1)
-            above = pltpu.roll(pltpu.roll(field, 127, 2), 7, 1)
-            field = field + jnp.where(takes_low, below, jnp.where(takes_high, above, 0.0))
-            out[half * LANES : (half + 1) * LANES, rows] = field.reshape(128, LANES).T
+            out[half * LANES : (half + 1) * LANES, rows] = raw[half, rows, :].T
 
     all_cost = group_send[...]
     for j in range(1, grp_count):
@@ -433,7 +462,6 @@
 
     for p in range(dev_count):
         when(p != d, lambda: data_copy(p, p).wait_send())
-        when(p != d, lambda: cost_copy(p, p).wait_send())
     for j in range(1, grp_count):
         group_copy(j).wait_send()
     for i in range(2):
@@ -473,25 +501,21 @@
             pltpu.VMEM((obs_rows, LANES), jnp.int32),
             pltpu.VMEM((obs_rows, LANES), jnp.int32),
             pltpu.VMEM((obs_rows, LANES), jnp.int32),
-            pltpu.VMEM((4, obs_rows, LANES), F32),
-            pltpu.VMEM((dev_count, CHANNELS * per_dest, LANES), F32),
-            pltpu.VMEM((dev_count, CHANNELS * per_dest, LANES), F32),
-            pltpu.VMEM((1, LANES), F32),
-            pltpu.VMEM((dev_count, 1, LANES), F32),
+            pltpu.VMEM((5, obs_rows, LANES), F32),
+            pltpu.VMEM((dev_count, CHANNELS * per_dest + 1, LANES), F32),
+            pltpu.VMEM((dev_count, CHANNELS * per_dest + 1, LANES), F32),
             pltpu.VMEM((1, LANES), F32),
             pltpu.VMEM((grp_count, 1, LANES), F32),
             pltpu.VMEM((64, batch_rows, LANES), F32),
             pltpu.VMEM((8 * batch_rows, LANES), F32),
             pltpu.VMEM((len(OUTER_PAIRS) * 8, ELEM_DEV), F32),
             pltpu.VMEM((len(INNER_PAIRS) * 8, ELEM_DEV), F32),
-            pltpu.VMEM((512, ELEM_DEV), F32),
+            pltpu.VMEM((2, 512, LANES), F32),
             pltpu.VMEM((2, 32, LANES), F32),
             pltpu.VMEM((2, 32, LANES), F32),
             pltpu.VMEM((2, 2, 8, LANES), F32),
             pltpu.VMEM((2, 2, 8, LANES), F32),
             pltpu.VMEM((2, 2, 8, LANES), F32),
-            dma((dev_count,)),
-            dma((dev_count,)),
             dma((dev_count,)),
             dma((dev_count,)),
             dma((grp_count,)),

time: 19.7 us -> 19.2 us (0.975)
  the two profiles are of different devices: /device:TPU:1 before, /device:TPU:17 now
where the time goes in v4:
time: 19.2 us; the launch traced here: 18.9 us
  Pallas kernels  16.3 us (85%)
  between operations  1.8 us (9%)
  local copies, waits for them, and re-layouts  0.8 us (4%)
    pallas_call x1, Pallas kernels, on_device(): pl.pallas_call(functools.partial(kernel, dev_count, grp_count, capacity),...  16.3 us
    unnamed x1, local copies, waits for them, and re-layouts  0.8 us

profile of v4, /device:TPU:17, one launch (start us, length us, event | category | flops | bytes accessed | tf_op | source)
XLA Modules:
  0.0 18.9 jit_solution(2344610064399091569)
XLA Ops:
  0.6 16.3 %shard_map.77 = (f32[256,512]{1,0:T(8,128)S(1)}, f32[1,128]{1,0:T(1,128)S(1)}) custom-call(f32[3,4096]{1,0:T(4,128)} %coord_in.1, f32[32,128]{1,0:T(8,128)} %bitcast.10, f32[32,128]{1,0:T(8,128)} %bitcast.11, s32[32,128]{1,0:T(8,128)} %bitcast.12, s32[32,128]{1,0:T(8,128)} %bitcast.13, s32[32,128]{1,0:T(8,128)} %bitcast.14), custom_call_target="tpu_custom_call" | custom-call | tf_op jit(solution)/shard_map/pallas_call | solution.py:489
  16.9 0.8 %copy.10 = f32[4,8,8,512]{3,2,1,0:T(8,128)} copy(f32[4,8,8,512]{3,2,1,0:T(8,128)S(1)} %bitcast.8) | data formatting | bytes 1048576

commit v5 on v4

--- a/solution.py
+++ b/solution.py
@@ -83,7 +83,7 @@
     outer, third, face_rows, inner_rows, raw, a_send, a_recv, b_send, b_recv, edge_recv,
     send_sem, recv_sem, group_send_sem, group_recv_sem,
     face_send_sem, face_recv_sem, edge_send_sem, edge_recv_sem, load_sem,
-    up_sem, others_sem,
+    up_sem, head_sem, ready_sem,
 ):
     g = lax.axis_index("grp")
     d = lax.axis_index("dev")
@@ -118,24 +118,18 @@
         load.start()
 
     barrier = pltpu.get_barrier_semaphore()
-    others = [wrapped(j, 0) for j in range(1, grp_count)]
-    others += [wrapped(i, j) for i in (-1, 1) for j in (-1, 1)]
-
     def signal(semaphore, partner):
         pl.semaphore_signal(semaphore, inc=1, device_id=partner, device_id_type=MESH)
 
-    def is_lower(partner):
-        return (partner[1] < d) | ((partner[1] == d) & (partner[0] < g))
-
+    heads = [wrapped(j, 0) for j in range(1, grp_count)]
     for p in range(dev_count):
         when(p > d, lambda: signal(barrier, (g, p)))
-    lower_count = d
-    higher_others = len(others)
-    for partner in others:
-        lower = is_lower(partner)
-        when(jnp.logical_not(lower), lambda: signal(barrier, partner))
-        lower_count = lower_count + lower.astype(jnp.int32)
-        higher_others = higher_others - lower.astype(jnp.int32)
+    for head in heads:
+        when(d == 0, lambda: signal(barrier, head))
+    pl.semaphore_wait(barrier, jnp.where(d == 0, len(heads), d))
+    for p in range(dev_count):
+        when(p < d, lambda: signal(up_sem.at[d], (g, p)))
+
     for load in loads:
         load.wait()
 
@@ -210,12 +204,6 @@
         data_copy(p, d).start()
 
     looped(lambda: pack(0))
-    when(lower_count > 0, lambda: pl.semaphore_wait(barrier, lower_count))
-    for p in range(dev_count):
-        when(p < d, lambda: signal(up_sem.at[d], (g, p)))
-    for partner in others:
-        when(is_lower(partner), lambda: signal(others_sem, partner))
-
     for p in range(half_dev):
         when(p < d, lambda: send_to(p))
     looped(lambda: pack(1))
@@ -223,12 +211,18 @@
         when(p < d, lambda: send_to(p))
     for i in range(batch):
         when(own * batch + i > d, lambda: send_to(own * batch + i))
+
+    def send_up(x):
+        for i in range(batch):
+            when(x < BATCHES, lambda: send_to(x * batch + i))
+
+    send_up(own + 1)
     recv[d] = send[d]
 
     elem_ids = sublane_ids(ELEM_DEV)
     rows = batch * per_dest
 
-    def prepare(x):
+    def prepare(x, t):
         def channel(c):
             start = c * per_dest
             parts = [recv[x * batch + i, start : start + per_dest, :] for i in range(batch)]
@@ -237,19 +231,19 @@
         weighted = [first * channel(3) for first in basis_values(channel(0))]
         second = basis_values(channel(1))
         for c, value in enumerate(basis_values(channel(2))):
-            third[c * rows : (c + 1) * rows, :] = value
+            third[t, c * rows : (c + 1) * rows, :] = value
         for i, (a, b) in enumerate(PAIRS):
-            outer[i] = weighted[a] * second[b]
-
-    def pair_sums(x, groups):
+            outer[t, i] = weighted[a] * second[b]
+
+    def pair_sums(x, t, groups):
         left, right = [], []
         for h in range(rows):
-            w = third[pl.ds(h, 8, stride=rows), :]
+            w = third[t, pl.ds(h, 8, stride=rows), :]
             pieces = []
             for start, stop in groups:
                 highs, lows = [], []
                 for i in range(start, stop, 2):
-                    value = jnp.concatenate([outer[k, h : h + 1, :] * w for k in (i, i + 1)], axis=0)
+                    value = jnp.concatenate([outer[t, k, h : h + 1, :] * w for k in (i, i + 1)], axis=0)
                     high = value.astype(BF16)
                     highs.append(high)
                     lows.append((value - high.astype(F32)).astype(BF16))
@@ -275,45 +269,58 @@
         when(own * batch + i != d, lambda: arrive(own * batch + i))
 
     def first_sums():
-        prepare(own)
-        face_rows[...], inner_rows[...] = pair_sums(own, (faces, inners))
+        prepare(own, 0)
+        face_rows[...], inner_rows[...] = pair_sums(own, 0, (faces, inners))
 
     looped(first_sums)
 
-    def send_up(x):
-        for i in range(batch):
-            when(x < BATCHES, lambda: send_to(x * batch + i))
-
-    send_up(own + 1)
-    send_up(own + 2)
-
-    def from_batch(t):
+    for j in range(2, BATCHES):
+        send_up(own + j)
+    for head in heads:
+        when(d == 0, lambda: signal(head_sem, head))
+
+    def batch_of(t):
         early = own < BATCHES // 2
         turn = jnp.where(early, own, BATCHES - 1 - own)
         x = t - 1 + (t > turn).astype(jnp.int32)
-        x = jnp.where(early, x, BATCHES - 1 - x)
+        return jnp.where(early, x, BATCHES - 1 - x)
+
+    def from_batch(t):
+        x = batch_of(t)
         for i in range(batch):
             arrive(x * batch + i)
-        prepare(x)
+        prepare(x, t)
         return x
 
-    def middle(t, carry):
-        for j in range(3, BATCHES):
-            when(t == j - 1, lambda: send_up(own + j))
-        face, inner = pair_sums(from_batch(t), (faces, inners))
+    def all_rows(t, carry):
+        face, inner = pair_sums(from_batch(t), t, (faces, inners))
         face_rows[...] += face
         inner_rows[...] += inner
         return carry
 
-    lax.fori_loop(1, BATCHES - 1, middle, 0)
+    def only_faces(t, carry):
+        face_rows[...] += pair_sums(from_batch(t), t, (faces,))[0]
+        return carry
+
+    def only_inner(t, carry):
+        inner_rows[...] += pair_sums(batch_of(t), t, (inners,))[0]
+        return carry
+
+    split = jnp.where(own == 0, BATCHES - 2, 1)
+    lax.fori_loop(1, split, all_rows, 0)
+
+    @pl.when(d == 0)
+    def _():
+        pl.semaphore_wait(head_sem, len(heads))
+        for p in range(1, dev_count):
+            signal(ready_sem, (g, p))
+
+    lax.fori_loop(split, BATCHES - 1, only_faces, 0)
     last = from_batch(BATCHES - 1)
-    when(higher_others > 0, lambda: pl.semaphore_wait(others_sem, higher_others))
     group_cost = recv[0, cost_row, :]
     for i in range(1, dev_count):
         group_cost = group_cost + recv[i, cost_row, :]
     group_send[...] = group_cost
-    for j in range(1, grp_count):
-        group_copy(j).start()
 
     def place(value, pairs):
         for i, (a, b) in enumerate(pairs):
@@ -322,7 +329,10 @@
                 lanes = slice(half * LANES, (half + 1) * LANES)
                 raw[half, start : start + 8, :] = value[i * 8 : i * 8 + 8, lanes]
 
-    looped(lambda: place(face_rows[...] + pair_sums(last, (faces,))[0], OUTER_PAIRS))
+    def last_faces():
+        place(face_rows[...] + pair_sums(last, BATCHES - 1, (faces,))[0], OUTER_PAIRS)
+
+    looped(last_faces)
 
     lane = lax.broadcasted_iota(jnp.int32, (1, LANES), 1)
     lower_half = lane < 64
@@ -368,6 +378,9 @@
     def clear(ref, i):
         ref[i] = jnp.zeros_like(ref[i])
 
+    when(d > 0, lambda: pl.semaphore_wait(ready_sem, 1))
+    for j in range(1, grp_count):
+        group_copy(j).start()
     for j in range(2):
         for i in range(2):
             when(sends_a[i] & sends_b[j], lambda: edge_copy(i, j).start())
@@ -375,7 +388,8 @@
         when(sends_a[i], lambda: face_copy(i).start())
         when(sends_b[i], lambda: face_copy(2 + i).start())
 
-    looped(lambda: place(inner_rows[...] + pair_sums(last, (inners,))[0], INNER_PAIRS))
+    lax.fori_loop(split, BATCHES, only_inner, 0)
+    place(inner_rows[...], INNER_PAIRS)
 
     low_rows, high_rows = slice(0, 64), slice(448, 512)
     low = [raw[half, low_rows, :] for half in range(2)]
@@ -506,8 +520,8 @@
             pltpu.VMEM((dev_count, CHANNELS * per_dest + 1, LANES), F32),
             pltpu.VMEM((1, LANES), F32),
             pltpu.VMEM((grp_count, 1, LANES), F32),
-            pltpu.VMEM((64, batch_rows, LANES), F32),
-            pltpu.VMEM((8 * batch_rows, LANES), F32),
+            pltpu.VMEM((BATCHES, 64, batch_rows, LANES), F32),
+            pltpu.VMEM((BATCHES, 8 * batch_rows, LANES), F32),
             pltpu.VMEM((len(OUTER_PAIRS) * 8, ELEM_DEV), F32),
             pltpu.VMEM((len(INNER_PAIRS) * 8, ELEM_DEV), F32),
             pltpu.VMEM((2, 512, LANES), F32),
@@ -527,6 +541,7 @@
             dma((6,)),
             regular((dev_count,)),
             regular,
+            regular,
         ],
         compiler_params=pltpu.CompilerParams(collective_id=0, has_side_effects=True),
     )(obs_coord, *rows)

time: 19.2 us -> 17.6 us (0.917)
  the two profiles are of different devices: /device:TPU:17 before, /device:TPU:1 now
where the time goes in v5:
time: 17.6 us; the launch traced here: 17.3 us
  Pallas kernels  14.7 us (84%)
  between operations  1.8 us (10%)
  local copies, waits for them, and re-layouts  0.8 us (5%)
    pallas_call x1, Pallas kernels, on_device(): pl.pallas_call(functools.partial(kernel, dev_count, grp_count, capacity),...  14.7 us
    unnamed x1, local copies, waits for them, and re-layouts  0.8 us

profile of v5, /device:TPU:1, one launch (start us, length us, event | category | flops | bytes accessed | tf_op | source)
XLA Modules:
  0.0 17.3 jit_solution(11245691713565678861)
XLA Ops:
  0.6 14.7 %shard_map.77 = (f32[256,512]{1,0:T(8,128)S(1)}, f32[1,128]{1,0:T(1,128)S(1)}) custom-call(f32[3,4096]{1,0:T(4,128)} %coord_in.1, f32[32,128]{1,0:T(8,128)} %bitcast.10, f32[32,128]{1,0:T(8,128)} %bitcast.11, s32[32,128]{1,0:T(8,128)} %bitcast.12, s32[32,128]{1,0:T(8,128)} %bitcast.13, s32[32,128]{1,0:T(8,128)} %bitcast.14), custom_call_target="tpu_custom_call" | custom-call | tf_op jit(solution)/shard_map/pallas_call | solution.py:503
  15.3 0.8 %copy.10 = f32[4,8,8,512]{3,2,1,0:T(8,128)} copy(f32[4,8,8,512]{3,2,1,0:T(8,128)S(1)} %bitcast.8) | data formatting | bytes 1048576

commit v6 on v5

--- a/solution.py
+++ b/solution.py
@@ -133,21 +133,7 @@
     for load in loads:
         load.wait()
 
-    residual = resid[...]
-    forcing = weight[...] * residual
-    where = dest[...]
-    which = slot[...]
-    row = where % quarter_dev * per_dest + which // LANES
-    for half in range(2):
-        terms[half] = jnp.where(where // half_dev == half, row, -1).astype(F32)
-    terms[2] = (where // quarter_dev % 2 * LANES + which % LANES).astype(F32)
-    terms[3] = forcing
-    terms[4] = elem[...].astype(F32)
-    part = jnp.sum(forcing * residual, axis=0, keepdims=True)
-    part = jnp.broadcast_to(0.5 * jnp.sum(part, axis=1, keepdims=True), (1, LANES))
     cost_row = slice(CHANNELS * per_dest, CHANNELS * per_dest + 1)
-    for p in range(dev_count):
-        send[p, cost_row, :] = part
 
     row_ids = sublane_ids(row_total)
     lane_ids = sublane_ids(2 * LANES, 32)
@@ -159,6 +145,22 @@
             return carry
 
         lax.fori_loop(0, once, step, 0)
+
+    def set_terms():
+        residual = resid[...]
+        forcing = weight[...] * residual
+        where = dest[...]
+        which = slot[...]
+        row = where % quarter_dev * per_dest + which // LANES
+        for half in range(2):
+            terms[half] = jnp.where(where // half_dev == half, row, -1).astype(F32)
+        terms[2] = (where // quarter_dev % 2 * LANES + which % LANES).astype(F32)
+        terms[3] = forcing
+        terms[4] = elem[...].astype(F32)
+        part = jnp.sum(forcing * residual, axis=0, keepdims=True)
+        part = jnp.broadcast_to(0.5 * jnp.sum(part, axis=1, keepdims=True), (1, LANES))
+        for p in range(dev_count):
+            send[p, cost_row, :] = part
 
     def pack(half):
         left, right = [], []
@@ -203,7 +205,11 @@
         when(p > d, lambda: pl.semaphore_wait(up_sem.at[p], 1))
         data_copy(p, d).start()
 
-    looped(lambda: pack(0))
+    def pack_first():
+        set_terms()
+        pack(0)
+
+    looped(pack_first)
     for p in range(half_dev):
         when(p < d, lambda: send_to(p))
     looped(lambda: pack(1))
@@ -219,7 +225,7 @@
     send_up(own + 1)
     recv[d] = send[d]
 
-    elem_ids = sublane_ids(ELEM_DEV)
+    elem_ids = sublane_ids(ELEM_DEV, 32)
     rows = batch * per_dest
 
     def prepare(x, t):
@@ -251,7 +257,8 @@
             left.append(jnp.concatenate(pieces, axis=0))
             start = 4 * per_dest + h % per_dest
             owner = recv[x * batch + h // per_dest, start : start + 1, :]
-            right.append(jnp.concatenate(one_hot(owner, elem_ids), axis=0))
+            hot = one_hot(owner, elem_ids)
+            right.append(jnp.concatenate([part.astype(F8) for part in hot], axis=0))
         total = dot_nt(jnp.concatenate(left, axis=1), jnp.concatenate(right, axis=1))
         sums, row = [], 0
         for start, stop in groups:
@@ -292,35 +299,29 @@
         prepare(x, t)
         return x
 
-    def all_rows(t, carry):
-        face, inner = pair_sums(from_batch(t), t, (faces, inners))
-        face_rows[...] += face
-        inner_rows[...] += inner
-        return carry
+    def tell_ready():
+        pl.semaphore_wait(head_sem, len(heads))
+        for p in range(1, dev_count):
+            signal(ready_sem, (g, p))
 
     def only_faces(t, carry):
         face_rows[...] += pair_sums(from_batch(t), t, (faces,))[0]
+        when((d == 0) & (t == 1), tell_ready)
         return carry
 
     def only_inner(t, carry):
         inner_rows[...] += pair_sums(batch_of(t), t, (inners,))[0]
         return carry
 
-    split = jnp.where(own == 0, BATCHES - 2, 1)
-    lax.fori_loop(1, split, all_rows, 0)
-
-    @pl.when(d == 0)
-    def _():
-        pl.semaphore_wait(head_sem, len(heads))
-        for p in range(1, dev_count):
-            signal(ready_sem, (g, p))
-
-    lax.fori_loop(split, BATCHES - 1, only_faces, 0)
+    lax.fori_loop(1, BATCHES - 1, only_faces, 0)
     last = from_batch(BATCHES - 1)
     group_cost = recv[0, cost_row, :]
     for i in range(1, dev_count):
         group_cost = group_cost + recv[i, cost_row, :]
     group_send[...] = group_cost
+    when(d > 0, lambda: pl.semaphore_wait(ready_sem, 1))
+    for j in range(1, grp_count):
+        group_copy(j).start()
 
     def place(value, pairs):
         for i, (a, b) in enumerate(pairs):
@@ -378,17 +379,14 @@
     def clear(ref, i):
         ref[i] = jnp.zeros_like(ref[i])
 
-    when(d > 0, lambda: pl.semaphore_wait(ready_sem, 1))
-    for j in range(1, grp_count):
-        group_copy(j).start()
-    for j in range(2):
-        for i in range(2):
+    for i in (1, 0):
+        for j in range(2):
             when(sends_a[i] & sends_b[j], lambda: edge_copy(i, j).start())
-    for i in range(2):
+    for i in (1, 0):
         when(sends_a[i], lambda: face_copy(i).start())
         when(sends_b[i], lambda: face_copy(2 + i).start())
 
-    lax.fori_loop(split, BATCHES, only_inner, 0)
+    lax.fori_loop(1, BATCHES, only_inner, 0)
     place(inner_rows[...], INNER_PAIRS)
 
     low_rows, high_rows = slice(0, 64), slice(448, 512)
@@ -419,17 +417,21 @@
         when(jnp.logical_not(gets_a[i]), lambda: clear(a_recv, i))
     for i in range(2):
         got = a_recv[i]
-        parts = [got, pltpu.roll(got, 64, 1)]
+        far = pltpu.roll(got, 64, 1)
+        start = i * 448
         if i == 0:
-            got = jnp.where(lower_half, jnp.concatenate(parts, axis=0), 0.0)
+            keep, low, high = lower_half, got[0:8], pltpu.roll(got[24:32], 72, 1)
+            low = pltpu.roll(low, 120, 1)
+            got = jnp.concatenate([got, far], axis=0)
         else:
-            got = jnp.where(lower_half, 0.0, jnp.concatenate(parts[::-1], axis=0))
-        start = i * 448
-        raw[i, start : start + 8, :] += got[0:8] + from_below(got[56:64])
+            keep, low, high = jnp.logical_not(lower_half), pltpu.roll(got[0:8], 56, 1), got[24:32]
+            high = pltpu.roll(high, 8, 1)
+            got = jnp.concatenate([far, got], axis=0)
+        got = jnp.where(keep, got, 0.0)
+        raw[i, start : start + 8, :] += got[0:8] + jnp.where(keep & (node > 0), high, 0.0)
         raw[i, start + 8 : start + 56, :] += got[8:56]
-        raw[i, start + 56 : start + 64, :] += got[56:64] + from_above(got[0:8])
-
-    faces = []
+        raw[i, start + 56 : start + 64, :] += got[56:64] + jnp.where(keep & (node < 7), low, 0.0)
+
     for j in range(2):
         when(gets_b[j], lambda: face_copy(2 + j).wait_recv())
         when(jnp.logical_not(gets_b[j]), lambda: clear(b_recv, j))
@@ -437,24 +439,19 @@
             both = gets_a[i] & gets_b[j]
             when(both, lambda: edge_copy(i, j).wait_recv())
             when(jnp.logical_not(both), lambda: clear(edge_recv, (j, i)))
-        first, second = b_recv[j, 0], b_recv[j, 1]
-        up = [pltpu.roll(x, 8, 1) for x in (edge_recv[j, 0], first, second)]
-        down = [pltpu.roll(x, 120, 1) for x in (first, second, edge_recv[j, 1])]
-        face = []
-        for half, own in enumerate((first, second)):
-            from_low = jnp.where(lower_half, up[half], up[half + 1])
-            from_high = jnp.where(lower_half, down[half], down[half + 1])
-            face.append(
-                own + jnp.where(node == 0, from_low, jnp.where(node == 7, from_high, 0.0))
-            )
-        faces.append(face)
-    for half in range(2):
-        for a in range(8):
-            low_rows, high_rows = slice(a * 64, a * 64 + 8), slice(a * 64 + 56, a * 64 + 64)
-            got_low = pltpu.roll(faces[0][half], (128 - a * 8) % 128, 1)
-            got_high = pltpu.roll(faces[1][half], (56 - a * 8) % 128, 1)
-            raw[half, low_rows, :] += jnp.where(node == 0, got_low, 0.0)
-            raw[half, high_rows, :] += jnp.where(node == 7, got_high, 0.0)
+    for j in range(2):
+        mine = [b_recv[j, 0], b_recv[j, 1]]
+        up = [pltpu.roll(x, (8, 64)[j], 1) for x in (edge_recv[j, 0], *mine)]
+        down = [pltpu.roll(x, (64, 120)[j], 1) for x in (*mine, edge_recv[j, 1])]
+        for half in range(2):
+            for a in range(8):
+                got = pltpu.roll(mine[half], (56 * j - a * 8) % 128, 1)
+                if a == 0:
+                    got = got + jnp.where(lower_half, up[half], up[half + 1])
+                if a == 7:
+                    got = got + jnp.where(lower_half, down[half], down[half + 1])
+                start = a * 64 + 56 * j
+                raw[half, start : start + 8, :] += jnp.where(node == 7 * j, got, 0.0)
 
     ez = lane % 8
     for half in range(2):

time: 17.6 us -> 17.3 us (0.983)
  Pallas kernels: 14.7 us -> 14.5 us
    pallas_call x1, Pallas kernels: 14.7 us -> 14.5 us  [on_device(): pl.pallas_call(functools.partial(kernel, dev_count, grp_count, capacity),...]
where the time goes in v6:
time: 17.3 us; the launch traced here: 17.1 us
  Pallas kernels  14.5 us (84%)
  between operations  1.8 us (10%)
  local copies, waits for them, and re-layouts  0.8 us (5%)
    pallas_call x1, Pallas kernels, on_device(): pl.pallas_call(functools.partial(kernel, dev_count, grp_count, capacity),...  14.5 us
    unnamed x1, local copies, waits for them, and re-layouts  0.8 us

profile of v6, /device:TPU:1, one launch (start us, length us, event | category | flops | bytes accessed | tf_op | source)
XLA Modules:
  0.0 17.1 jit_solution(12551792731189128965)
XLA Ops:
  0.6 14.5 %shard_map.77 = (f32[256,512]{1,0:T(8,128)S(1)}, f32[1,128]{1,0:T(1,128)S(1)}) custom-call(f32[3,4096]{1,0:T(4,128)} %coord_in.1, f32[32,128]{1,0:T(8,128)} %bitcast.10, f32[32,128]{1,0:T(8,128)} %bitcast.11, s32[32,128]{1,0:T(8,128)} %bitcast.12, s32[32,128]{1,0:T(8,128)} %bitcast.13, s32[32,128]{1,0:T(8,128)} %bitcast.14), custom_call_target="tpu_custom_call" | custom-call | tf_op jit(solution)/shard_map/pallas_call | solution.py:500
  15.1 0.8 %copy.10 = f32[4,8,8,512]{3,2,1,0:T(8,128)} copy(f32[4,8,8,512]{3,2,1,0:T(8,128)S(1)} %bitcast.8) | data formatting | bytes 1048576

commit v7 on v6

--- a/solution.py
+++ b/solution.py
@@ -82,7 +82,7 @@
     group_send, group_recv,
     outer, third, face_rows, inner_rows, raw, a_send, a_recv, b_send, b_recv, edge_recv,
     send_sem, recv_sem, group_send_sem, group_recv_sem,
-    face_send_sem, face_recv_sem, edge_send_sem, edge_recv_sem, load_sem,
+    face_send_sem, face_recv_sem, edge_send_sem, edge_recv_sem,
     up_sem, head_sem, ready_sem,
 ):
     g = lax.axis_index("grp")
@@ -106,7 +106,7 @@
         )
 
     loads = [
-        pltpu.make_async_copy(source, sink, load_sem.at[i])
+        pltpu.make_async_copy(source, sink, send_sem.at[i])
         for i, (source, sink) in enumerate(
             zip(
                 (dest_in, slot_in, resid_in, weight_in, coord_in, elem_in),
@@ -228,22 +228,23 @@
     elem_ids = sublane_ids(ELEM_DEV, 32)
     rows = batch * per_dest
 
-    def prepare(x, t):
+    def prepare(x, t, begin=0, end=batch):
         def channel(c):
             start = c * per_dest
-            parts = [recv[x * batch + i, start : start + per_dest, :] for i in range(batch)]
+            parts = [recv[x * batch + i, start : start + per_dest, :] for i in range(begin, end)]
             return jnp.concatenate(parts, axis=0)
 
-        weighted = [first * channel(3) for first in basis_values(channel(0))]
+        first, last = begin * per_dest, end * per_dest
+        weighted = [value * channel(3) for value in basis_values(channel(0))]
         second = basis_values(channel(1))
         for c, value in enumerate(basis_values(channel(2))):
-            third[t, c * rows : (c + 1) * rows, :] = value
+            third[t, c * rows + first : c * rows + last, :] = value
         for i, (a, b) in enumerate(PAIRS):
-            outer[t, i] = weighted[a] * second[b]
-
-    def pair_sums(x, t, groups):
+            outer[t, i, first:last] = weighted[a] * second[b]
+
+    def pair_sums(x, t, groups, begin=0, end=batch):
         left, right = [], []
-        for h in range(rows):
+        for h in range(begin * per_dest, end * per_dest):
             w = third[t, pl.ds(h, 8, stride=rows), :]
             pieces = []
             for start, stop in groups:
@@ -412,6 +413,22 @@
             raw[half, low_rows, :] = low + from_below(high)
             raw[half, high_rows, :] = high + from_above(low)
 
+    all_cost = group_send[...]
+    for j in range(1, grp_count):
+        group_copy(j).wait_recv()
+        all_cost = all_cost + group_recv[j]
+    cost[...] = all_cost
+
+    for p in range(dev_count):
+        when(p != d, lambda: data_copy(p, p).wait_send())
+    for j in range(1, grp_count):
+        group_copy(j).wait_send()
+    for i in range(2):
+        when(sends_a[i], lambda: face_copy(i).wait_send())
+        when(sends_b[i], lambda: face_copy(2 + i).wait_send())
+        for j in range(2):
+            when(sends_a[i] & sends_b[j], lambda: edge_copy(i, j).wait_send())
+
     for i in range(2):
         when(gets_a[i], lambda: face_copy(i).wait_recv())
         when(jnp.logical_not(gets_a[i]), lambda: clear(a_recv, i))
@@ -464,22 +481,6 @@
         for part in range(4):
             rows = slice(part * 128, (part + 1) * 128)
             out[half * LANES : (half + 1) * LANES, rows] = raw[half, rows, :].T
-
-    all_cost = group_send[...]
-    for j in range(1, grp_count):
-        group_copy(j).wait_recv()
-        all_cost = all_cost + group_recv[j]
-    cost[...] = all_cost
-
-    for p in range(dev_count):
-        when(p != d, lambda: data_copy(p, p).wait_send())
-    for j in range(1, grp_count):
-        group_copy(j).wait_send()
-    for i in range(2):
-        when(sends_a[i], lambda: face_copy(i).wait_send())
-        when(sends_b[i], lambda: face_copy(2 + i).wait_send())
-        for j in range(2):
-            when(sends_a[i] & sends_b[j], lambda: edge_copy(i, j).wait_send())
 
 
 def on_device(obs_coord, obs_resid, obs_weight, obs_dest, obs_send_slot, obs_elem, obs_slot):
@@ -535,7 +536,6 @@
             dma((4,)),
             dma((2, 2)),
             dma((2, 2)),
-            dma((6,)),
             regular((dev_count,)),
             regular,
             regular,

time: 17.3 us -> 17.2 us (level)
  no operation moved by 1% of the time
where the time goes in v7:
time: 17.2 us; the launch traced here: 17 us
  Pallas kernels  14.4 us (84%)
  between operations  1.8 us (10%)
  local copies, waits for them, and re-layouts  0.8 us (5%)
    pallas_call x1, Pallas kernels, on_device(): pl.pallas_call(functools.partial(kernel, dev_count, grp_count, capacity),...  14.4 us
    unnamed x1, local copies, waits for them, and re-layouts  0.8 us

profile of v7, /device:TPU:1, one launch (start us, length us, event | category | flops | bytes accessed | tf_op | source)
XLA Modules:
  0.0 17.0 jit_solution(1942451223220114260)
XLA Ops:
  0.6 14.4 %shard_map.77 = (f32[256,512]{1,0:T(8,128)S(1)}, f32[1,128]{1,0:T(1,128)S(1)}) custom-call(f32[3,4096]{1,0:T(4,128)} %coord_in.1, f32[32,128]{1,0:T(8,128)} %bitcast.10, f32[32,128]{1,0:T(8,128)} %bitcast.11, s32[32,128]{1,0:T(8,128)} %bitcast.12, s32[32,128]{1,0:T(8,128)} %bitcast.13, s32[32,128]{1,0:T(8,128)} %bitcast.14), custom_call_target="tpu_custom_call" | custom-call | tf_op jit(solution)/shard_map/pallas_call | solution.py:501
  15.0 0.8 %copy.10 = f32[4,8,8,512]{3,2,1,0:T(8,128)} copy(f32[4,8,8,512]{3,2,1,0:T(8,128)S(1)} %bitcast.8) | data formatting | bytes 1048576

commit v8 on v7

--- a/solution.py
+++ b/solution.py
@@ -339,10 +339,6 @@
     lane = lax.broadcasted_iota(jnp.int32, (1, LANES), 1)
     lower_half = lane < 64
     node = (lane // 8) % 8
-    block = raw[1, 448:512, :]
-    a_send[0] = jnp.where(lower_half, pltpu.roll(block[0:32], 64, 1), block[32:64])
-    block = raw[0, 0:64, :]
-    a_send[1] = jnp.where(lower_half, block[0:32], pltpu.roll(block[32:64], 64, 1))
     for half in range(2):
         up = pltpu.roll(raw[half, 56:64, :], 72, 1)
         down = raw[half, 0:8, :]
@@ -383,6 +379,10 @@
     for i in (1, 0):
         for j in range(2):
             when(sends_a[i] & sends_b[j], lambda: edge_copy(i, j).start())
+    block = raw[1, 448:512, :]
+    a_send[0] = jnp.where(lower_half, pltpu.roll(block[0:32], 64, 1), block[32:64])
+    block = raw[0, 0:64, :]
+    a_send[1] = jnp.where(lower_half, block[0:32], pltpu.roll(block[32:64], 64, 1))
     for i in (1, 0):
         when(sends_a[i], lambda: face_copy(i).start())
         when(sends_b[i], lambda: face_copy(2 + i).start())

time: 17.2 us -> 17.2 us (level)
  no operation moved by 1% of the time
where the time goes in v8:
time: 17.2 us; the launch traced here: 17 us
  Pallas kernels  14.4 us (84%)
  between operations  1.8 us (10%)
  local copies, waits for them, and re-layouts  0.8 us (5%)
    pallas_call x1, Pallas kernels, on_device(): pl.pallas_call(functools.partial(kernel, dev_count, grp_count, capacity),...  14.4 us
    unnamed x1, local copies, waits for them, and re-layouts  0.8 us

profile of v8, /device:TPU:1, one launch (start us, length us, event | category | flops | bytes accessed | tf_op | source)
XLA Modules:
  0.0 17.0 jit_solution(15739051310155833496)
XLA Ops:
  0.6 14.4 %shard_map.77 = (f32[256,512]{1,0:T(8,128)S(1)}, f32[1,128]{1,0:T(1,128)S(1)}) custom-call(f32[3,4096]{1,0:T(4,128)} %coord_in.1, f32[32,128]{1,0:T(8,128)} %bitcast.10, f32[32,128]{1,0:T(8,128)} %bitcast.11, s32[32,128]{1,0:T(8,128)} %bitcast.12, s32[32,128]{1,0:T(8,128)} %bitcast.13, s32[32,128]{1,0:T(8,128)} %bitcast.14), custom_call_target="tpu_custom_call" | custom-call | tf_op jit(solution)/shard_map/pallas_call | solution.py:501
  15.0 0.8 %copy.10 = f32[4,8,8,512]{3,2,1,0:T(8,128)} copy(f32[4,8,8,512]{3,2,1,0:T(8,128)S(1)} %bitcast.8) | data formatting | bytes 1048576
